TPU v7x, 32 devices: a whole 2x2x4 slice. The times are simulated.
32 devices in a mesh: dp: 4 (over y, core), fsdp: 8 (over z, x).
Axes of the slice: x: 2, y: 2, z: 4, core: 2. Of those that a mesh axis runs over, the one named last changes fastest.
Arguments:
- states: bfloat16 [32, 1024, 512], P(('dp', 'fsdp')), may hold values from -6 to 6
- params: float32 [3150848], P(('dp', 'fsdp')), may hold values from -2 to 2
- first_moment: float32 [3150848], P(('dp', 'fsdp')), may hold values from -2 to 2
- second_moment: float32 [3150848], P(('dp', 'fsdp')), may hold values from 0.001 to 0.064
- ema_params: float32 [3150848], P(('dp', 'fsdp')), may hold values from -2 to 2
- lengths: int32 [32], P(('dp', 'fsdp')), may hold values from 64 to 1024, as said below
- halt_counts: int32 [32, 1024], P(('dp', 'fsdp')), may hold values from 1 to 2
- cotangent: bfloat16 [32, 1024, 512], P(('dp', 'fsdp')), may hold values from -6 to 6
Outputs:
- final_states: float32 [32, 1024, 512], P(('dp', 'fsdp'))
- input_grad: float32 [32, 1024, 512], P(('dp', 'fsdp'))
- param_grad: float32 [3150848], P(('dp', 'fsdp'))
- grad_norm: float32 [1], replicated
- new_params: float32 [3150848], P(('dp', 'fsdp'))
- new_first: float32 [3150848], P(('dp', 'fsdp'))
- new_second: float32 [3150848], P(('dp', 'fsdp'))
- new_ema: float32 [3150848], P(('dp', 'fsdp'))
- params_low: bfloat16 [3150848], P(('dp', 'fsdp'))
Inputs may be any that keep to these rules, and one draw needn't show every extreme that they name: `lengths`: some row is exactly 1024 long and another exactly 64.
All inputs are finite; a program needn't handle non-finite values.
Results may differ from a plain program's by a relative error of at most 0.011.
Values may be sent and summed in bfloat16 or wider, within the bound.
No kernel may reach another device: no remote copies, remote signals or barrier semaphores. Data moves between devices by JAX's collectives and lax.ppermute only.
A program may use at most 384 MiB of HBM per device.

v0:
```python
import functools
import math

import jax
import jax.numpy as jnp
import numpy as np
from jax import lax
from jax.experimental import pallas as pl
from jax.experimental.pallas import tpu as pltpu
from jax.sharding import PartitionSpec as P

D = 512
FF = 2048
HEADS = 8
SEQ = 1024
ADAM_STEP = 4
QKV_END = 786432
OUT_END = 1048576
UP_END = 2097152
DOWN_END = 3145728
NPARAM = 3150848

NORM_EPSILON = 1e-05
HALT_SHIFT = -1.0
BETA_FIRST = 0.9
BETA_SECOND = 0.999
ADAM_EPSILON = 1e-08
EMA_DECAY = 0.999
WEIGHT_DECAY = 0.1
RATE_MATRIX = 0.1
RATE_VECTOR = 1.0

BLOCK = 256
BLOCKS = SEQ // BLOCK
UNIT = 128
SIZES_LENGTH = (512,)
SIZES_ATTEND = (256, 128)
SIZES_SHIFTED = (128,)
SIZES_ATTEND_BACK = (256, 128)
SIZES_FEED = (512, 128)
SIZES_BACK = (512, 128)
PAIRS = HEADS // 2
PAIR = 128
SCORE_SCALE = 0.125
SCORE_LOG2 = SCORE_SCALE * math.log2(math.e)

f32 = jnp.float32
bf16 = jnp.bfloat16
i32 = jnp.int32

CHUNK = 192
DEVICES = 32
ROWS_A = 64
ROWS_B = 144
EXTRA = 16
PACKED = CHUNK + EXTRA
PLANE = [(0, 0), (1, 0), (0, 1), (1, 1)]
UP_SEGMENTS = [(0, 16, 0)] + [(64 + CHUNK * n, 48, 16 + 48 * n) for n in range(10)] + [(64 + CHUNK * 10, 16, 496)]


def dot(left, right):
    return jnp.dot(left, right, preferred_element_type=f32)


def dot_nt(left, right):
    return lax.dot_general(left, right, (((1,), (1,)), ((), ())), preferred_element_type=f32)


def dot_tn(left, right):
    return lax.dot_general(left, right, (((0,), (0,)), ((), ())), preferred_element_type=f32)


def iota(shape, axis):
    return lax.broadcasted_iota(i32, shape, axis)


def normalize(inputs):
    centred = inputs - jnp.mean(inputs, axis=-1, keepdims=True)
    rho = lax.rsqrt(jnp.mean(centred * centred, axis=-1, keepdims=True) + NORM_EPSILON)
    return centred * rho, rho


def norm_backward(grad_out, hat, rho, gain):
    grad_hat = grad_out * gain
    return rho * (
        grad_hat
        - jnp.mean(grad_hat, axis=-1, keepdims=True)
        - hat * jnp.mean(grad_hat * hat, axis=-1, keepdims=True)
    )


def gelu_parts(pre):
    cumulative = 0.5 + 0.5 * lax.erf(pre * 0.7071067811865476)
    density = jnp.exp2(pre * pre * (-0.5 * math.log2(math.e))) * 0.3989422804014327
    return pre * cumulative, cumulative + pre * density


def qkv_weight(ref, j):
    return jnp.concatenate([ref[CHUNK * n + 64 * j : CHUNK * n + 64 * (j + 1), :] for n in range(8)], axis=0)


def up_weight(ref, j):
    return jnp.concatenate(
        [ref[2048 + at + rows * j : 2048 + at + rows * (j + 1), :] for at, rows, _ in UP_SEGMENTS], axis=0
    )


def prepare_kernel(
    length_ref, index_ref, count_ref, state_ref, cotangent_ref, place_ref, states_out, cotangent_out, meta_ref
):
    length = length_ref[0]
    token = iota((1, SEQ), 1)
    valid = token < length
    two = jnp.where(valid & (count_ref[...] >= 2), 1.0, 0.0)
    one = jnp.where(valid & (count_ref[...] < 2), 1.0, 0.0)
    masks = jnp.concatenate([two, one, jnp.zeros((6, SEQ), f32)], axis=0).astype(bf16)
    earlier = jnp.where(iota((SEQ, SEQ), 0) < iota((SEQ, SEQ), 1), 1.0, 0.0).astype(bf16)
    ranks = dot(masks, earlier)
    n_two = jnp.sum(two)
    place = jnp.where(
        two > 0.0, ranks[0:1, :], jnp.where(one > 0.0, n_two + ranks[1:2, :], token.astype(f32))
    )
    place_ref[...] = jnp.broadcast_to(place, (8, SEQ))
    meta_ref[0] = n_two.astype(i32)
    meta_ref[1] = length
    for n in range(4):
        meta_ref[2 + n] = index_ref[n]

    def sort(block, carried):
        rows = pl.ds(pl.multiple_of(block * BLOCK, BLOCK), BLOCK)
        pick = jnp.where((iota((BLOCK, SEQ), 0) + block * BLOCK).astype(f32) == place, 1.0, 0.0).astype(bf16)
        states_out[rows, :] = dot(pick, state_ref[...]).astype(bf16)
        cotangent_out[rows, :] = dot(pick, cotangent_ref[...]).astype(bf16)
        return carried

    lax.fori_loop(0, BLOCKS, sort, 0)


def prepare(lengths, place_index, counts, states, cotangent):
    return pl.pallas_call(
        prepare_kernel,
        out_shape=(
            jax.ShapeDtypeStruct((8, SEQ), f32),
            jax.ShapeDtypeStruct((SEQ, D), bf16),
            jax.ShapeDtypeStruct((SEQ, D), bf16),
            jax.ShapeDtypeStruct((6,), i32),
        ),
        in_specs=[
            pl.BlockSpec(memory_space=pltpu.SMEM),
            pl.BlockSpec(memory_space=pltpu.SMEM),
            pl.BlockSpec(memory_space=pltpu.VMEM),
            pl.BlockSpec(memory_space=pltpu.VMEM),
            pl.BlockSpec(memory_space=pltpu.VMEM),
        ],
        out_specs=(
            pl.BlockSpec(memory_space=pltpu.VMEM),
            pl.BlockSpec(memory_space=pltpu.VMEM),
            pl.BlockSpec(memory_space=pltpu.VMEM),
            pl.BlockSpec(memory_space=pltpu.SMEM),
        ),
        cost_estimate=pl.CostEstimate(flops=6 * 10**9, transcendentals=0, bytes_accessed=4 * 10**6),
        name="prepare",
    )(lengths, place_index, counts, states, cotangent)


def restore_kernel(place_ref, sorted_ref, out_ref, columns, high, lower):
    columns[...] = jnp.broadcast_to(place_ref[0:1, :], (PAIR, SEQ)).T
    high[...] = sorted_ref[...].astype(bf16)
    lower[...] = (sorted_ref[...] - high[...].astype(f32)).astype(bf16)

    def unsort(block, carried):
        rows = pl.ds(pl.multiple_of(block * BLOCK, BLOCK), BLOCK)
        pick = jnp.concatenate(
            [
                jnp.where(columns[rows, :] == (iota((BLOCK, PAIR), 1) + PAIR * n).astype(f32), 1.0, 0.0).astype(bf16)
                for n in range(SEQ // PAIR)
            ],
            axis=1,
        )
        out_ref[rows, :] = dot(pick, high[...]) + dot(pick, lower[...])
        return carried

    lax.fori_loop(0, BLOCKS, unsort, 0)


def restore(place, array, name):
    return pl.pallas_call(
        restore_kernel,
        out_shape=jax.ShapeDtypeStruct((SEQ, D), f32),
        in_specs=[pl.BlockSpec(memory_space=pltpu.VMEM)] * 2,
        out_specs=pl.BlockSpec(memory_space=pltpu.VMEM),
        scratch_shapes=[pltpu.VMEM((SEQ, PAIR), f32), pltpu.VMEM((SEQ, D), bf16), pltpu.VMEM((SEQ, D), bf16)],
        cost_estimate=pl.CostEstimate(flops=6 * 10**9, transcendentals=0, bytes_accessed=4 * 10**6),
        name=name,
    )(place, array)


def next_rows(chunk, qkv_sum, out_sum, up_sum, packed, vector_sum):
    after = chunk + 1
    if after == DEVICES:
        return vector_sum[...]
    if after < 8:
        blocks = [qkv_sum[j, 64 * after : 64 * after + 8, :] for j in range(3)]
    elif after < 11:
        at = CHUNK * after - 1536
        return out_sum[at : at + 16, :]
    elif after < 22:
        first = 16 + 48 * (after - 11)
        blocks = [up_sum[j, first : first + 8, :] for j in range(4)]
    else:
        return packed[PACKED * after : PACKED * after + 16, :].astype(f32)
    width = len(blocks)
    rows = [blocks[r % width][r // width : r // width + 1, :] for r in range(10)]
    return jnp.concatenate(rows + [jnp.zeros((6, D), f32)], axis=0)


def chunk_of(meta, dy, dc, dz, dx):
    return (((meta[2] ^ dy) * 2 + (meta[3] ^ dc)) * 4 + (meta[4] ^ dz)) * 2 + (meta[5] ^ dx)


def shape_of(*shape, dtype=f32):
    return jax.ShapeDtypeStruct(shape, dtype)


def column_sum(array):
    return jnp.sum(array, axis=0, keepdims=True)


def layer_kernel(meta, states_ref, cotangent_ref, *refs):
    pieces = refs[:16]
    (
        final_out, carry, keep_a, send_a, keep_b, send_b, spill,
        matrices, extras, vectors,
        state, projected, mixed, middle, hidden, mixed_grad, projected_grad, logs, centres,
        qkv_sum, out_sum, up_sum, down_sum, vector_sum, first_key, norm_peak, key_sum, value_sum, turned, in_sem, spill_sem, out_sem,
    ) = refs[16:]
    n_two, length = meta[0], meta[1]
    lower = iota((1, PAIR), 1) < 64
    own = [lower, ~lower]

    def at_rows(start, size):
        return pl.ds(pl.multiple_of(start, UNIT), size)

    def hidden_rows(j, start, size):
        return pl.ds(pl.multiple_of(j * SEQ + start, UNIT), size)

    def over_rows(rows, sizes, body):
        def loop(first, size, count):
            def step(n, carried):
                body(first + n * size, size)
                return carried

            lax.fori_loop(0, count, step, 0)
            return first + count * size

        large = sizes[0]
        if len(sizes) == 1:
            return loop(0, large, (rows + large - 1) // large)
        covered = loop(0, large, (rows + large // 2 - 1) // large)
        return loop(covered, sizes[1], (jnp.maximum(rows - covered, 0) + sizes[1] - 1) // sizes[1])

    def rest_rows(covered, body):
        def step(n, carried):
            body(n * UNIT, UNIT)
            return carried

        lax.fori_loop(covered // UNIT, SEQ // UNIT, step, 0)

    def weight_qkv(j):
        return qkv_weight(matrices, j)

    def weight_out():
        return matrices[1536:2048, :]

    def weight_up(j):
        return up_weight(matrices, j)

    def weight_down(j):
        return matrices[4096 + D * j : 4096 + D * (j + 1), :]

    def vector(index):
        return vectors[index : index + 1, :]

    def add_vector(index, value):
        vector_sum[index : index + 1, :] += value

    def query_rows(step):
        return jnp.where(step == 0, length, n_two)

    def row_index(start, size):
        return iota((size, 1), 0) + start

    arriving = []
    for dc in range(2):
        for plane, (dy, dx) in enumerate(PLANE):
            for dz in range(4):
                chunk = chunk_of(meta, dy, dc, dz, dx)
                row = pl.multiple_of(chunk * CHUNK, CHUNK)
                part_a, part_b = pieces[4 * dc + dz].at[plane], pieces[8 + 4 * dc + plane].at[dz]
                for source, target in (
                    (part_a, matrices.at[pl.ds(row, ROWS_A), :]),
                    (part_b.at[: CHUNK - ROWS_A, :], matrices.at[pl.ds(row + ROWS_A, CHUNK - ROWS_A), :]),
                    (part_b.at[CHUNK - ROWS_A :, :], extras.at[chunk]),
                ):
                    copy = pltpu.make_async_copy(source, target, in_sem.at[len(arriving)])
                    copy.start()
                    arriving.append(copy)

    for total in (qkv_sum, out_sum, up_sum, down_sum, vector_sum):
        total[...] = jnp.zeros_like(total)

    mixed[...] = jnp.zeros_like(mixed)
    state[0] = states_ref[...].astype(f32)
    state[1] = jnp.zeros((SEQ, D), f32)
    for copy in arriving:
        copy.wait()

    def complete(row, value):
        rows = value.shape[0]
        matrices[row : row + rows, :] = (matrices[row : row + rows, :].astype(f32) + value).astype(bf16)

    for n in range(1, DEVICES):
        value = extras[n - 1].astype(f32)
        if n < 8 or 11 <= n < 22:
            width, stride = (3, 64) if n < 8 else (4, 48 if n < 21 else 16)
            for j in range(width):
                rows = jnp.concatenate([value[4 * j : 4 * j + 4, :], jnp.zeros((4, D), f32)], axis=0)
                complete(CHUNK * n + stride * j, rows)
        else:
            complete(CHUNK * n, value)
    vectors[...] = extras[DEVICES - 1].astype(f32)

    heads = jnp.where(iota((D, PAIR), 0) // 64 == iota((D, PAIR), 1), 1.0, 0.0).astype(bf16)

    def project(step):
        def body(start, size):
            rows = at_rows(start, size)
            hat, _ = normalize(state[step, rows, :])
            normed_low = (hat * vector(0) + vector(1)).astype(bf16)
            queries = dot(normed_low, weight_qkv(0))
            projected[step, rows, 0:D] = queries.astype(bf16)
            keys = dot(normed_low, weight_qkv(1))
            for index, array in enumerate((queries, keys)):
                norms = dot((array * array).astype(bf16), heads)
                norm_peak[index : index + 1, :] = jnp.maximum(
                    norm_peak[index : index + 1, :], jnp.max(norms, axis=0, keepdims=True)
                )

            @pl.when(start == 0)
            def _():
                first_key[...] = jnp.broadcast_to(keys[0:1, :], first_key.shape)

            inside = row_index(start, size) < length
            projected[step, rows, D : 2 * D] = jnp.where(inside, keys, first_key[0:1, :]).astype(bf16)
            values = dot(normed_low, weight_qkv(2))
            projected[step, rows, 2 * D : 3 * D] = jnp.where(inside, values, 0.0).astype(bf16)

        def fill(start, size):
            rows = at_rows(start, size)
            projected[step, rows, D : 2 * D] = jnp.broadcast_to(first_key[0:1, :], (size, D)).astype(bf16)
            projected[step, rows, 2 * D : 3 * D] = jnp.zeros((size, D), bf16)

        norm_peak[...] = jnp.zeros_like(norm_peak)
        rest_rows(over_rows(length, SIZES_LENGTH, body), fill)

    def attend_pair(step, start, size, pair, shifted):
        rows = at_rows(start, size)
        ones = jnp.where(iota((SEQ, 1), 0) < length, 1.0, 0.0).astype(bf16)
        queries = projected[step, rows, pl.ds(pair * PAIR, PAIR)]
        keys = projected[step, :, pl.ds(D + pair * PAIR, PAIR)]
        values = projected[step, :, pl.ds(2 * D + pair * PAIR, PAIR)]
        peaks, sums = [], []
        for half in range(2):
            scores = dot_nt(jnp.where(own[half], queries, jnp.zeros_like(queries)), keys) * SCORE_LOG2
            if shifted:
                peaks.append(jnp.max(scores, axis=-1, keepdims=True))
                scores = scores - peaks[half]
            sums.append(dot(jnp.exp2(scores).astype(bf16), jnp.where(own[half], values, ones)))
        total = jnp.where(lower, pltpu.roll(sums[0], 64, 1), pltpu.roll(sums[1], 64, 1))
        mixed[step, rows, pl.ds(pair * PAIR, PAIR)] = (jnp.where(lower, sums[0], sums[1]) / total).astype(bf16)
        log = jnp.log2(total)
        if shifted:
            log = log + jnp.where(lower, peaks[0], peaks[1])
        log = log.T
        for unit in range(size // UNIT):
            columns = slice(unit * UNIT, (unit + 1) * UNIT)
            logs[step, start // UNIT + unit, pl.ds(2 * pair, 1), :] = log[0:1, columns]
            logs[step, start // UNIT + unit, pl.ds(2 * pair + 1, 1), :] = log[64:65, columns]

    def attend(step):
        bound = jnp.max(norm_peak[0:1, :] * norm_peak[1:2, :])
        plain = bound * (1.02 * SCORE_LOG2) ** 2 < 60.0**2

        @pl.when(plain)
        def _():
            def body(start, size):
                for pair in range(PAIRS):
                    attend_pair(step, start, size, pair, False)

            over_rows(query_rows(step), SIZES_ATTEND, body)

        @pl.when(~plain)
        def _():
            def body(start, size):
                def each(pair, carried):
                    attend_pair(step, start, size, pl.multiple_of(pair, 1), True)
                    return carried

                lax.fori_loop(0, PAIRS, each, 0)

            over_rows(query_rows(step), SIZES_SHIFTED, body)

    def feed_forward(step):
        def body(start, size):
            rows = at_rows(start, size)
            between = state[step, rows, :] + dot(mixed[step, rows, :], weight_out())
            middle[step, rows, :] = between
            hat, _ = normalize(between)
            normed_low = (hat * vector(2) + vector(3)).astype(bf16)
            output = between + vector(4)
            for j in range(4):
                value, slope = gelu_parts(dot(normed_low, weight_up(j)) + vector(6 + j))
                value_low = value.astype(bf16)
                hidden[hidden_rows(j, start, size), :] = value_low
                hidden[hidden_rows(4 + j, start, size), :] = slope.astype(bf16)
                output = output + dot(value_low, weight_down(j))
            state[step + 1, rows, :] = output

        over_rows(query_rows(step), SIZES_FEED, body)

    def save():
        return pltpu.make_async_copy(hidden, spill, spill_sem)

    def fetch():
        return pltpu.make_async_copy(spill, hidden, spill_sem)

    def forward(step, carried):
        project(step)
        attend(step)

        @pl.when(step == 1)
        def _():
            save().wait()

        feed_forward(step)

        @pl.when(step == 0)
        def _():
            save().start()

        return carried

    lax.fori_loop(0, 2, forward, 0)

    def mix(start, size):
        rows = at_rows(start, size)
        row = row_index(start, size)
        two, valid = row < n_two, row < length
        before = state[1, rows, :]
        after = jnp.where(two, state[2, rows, :], before)
        halting = jax.nn.sigmoid(jnp.sum(before * vector(5), axis=-1, keepdims=True) + HALT_SHIFT)
        share_one = jnp.where(two, halting, 1.0)
        share_two = jnp.where(two, 1.0 - halting, 0.0)
        final_out[rows, :] = jnp.where(valid, share_one * before + share_two * after, 0.0)
        grad_final = jnp.where(valid, cotangent_ref[rows, :].astype(f32), 0.0)
        first_sum = jnp.sum(grad_final * before, axis=-1, keepdims=True)
        second_sum = jnp.sum(grad_final * after, axis=-1, keepdims=True)
        logit_grad = jnp.where(two, (first_sum - second_sum) * halting * (1.0 - halting), 0.0)
        add_vector(5, column_sum(jnp.where(valid, logit_grad * before, 0.0)))
        carry[rows, :] = share_two * grad_final
        state[2, rows, :] = jnp.where(valid, share_one * grad_final + logit_grad * vector(5), 0.0)

    def blank(start, size):
        rows = at_rows(start, size)
        final_out[rows, :] = jnp.zeros((size, D), f32)
        carry[rows, :] = jnp.zeros((size, D), f32)

    rest_rows(over_rows(length, SIZES_LENGTH, mix), blank)

    def feed_back(step):
        def body(start, size):
            rows = at_rows(start, size)
            grad = carry[rows, :]
            branch = grad.astype(bf16)
            add_vector(4, column_sum(branch.astype(f32)))
            hat, rho = normalize(middle[step, rows, :])
            normed_low = (hat * vector(2) + vector(3)).astype(bf16)
            normed_grad = jnp.zeros((size, D), f32)
            for j in range(4):
                down_sum[j] += dot_tn(branch, hidden[hidden_rows(j, start, size), :])
                slope = hidden[hidden_rows(4 + j, start, size), :].astype(f32)
                pre_grad = (dot_nt(branch, weight_down(j)) * slope).astype(bf16)
                add_vector(6 + j, column_sum(pre_grad.astype(f32)))
                up_sum[j] += dot_tn(normed_low, pre_grad)
                normed_grad = normed_grad + dot_nt(pre_grad, weight_up(j))
            add_vector(2, column_sum(normed_grad * hat))
            add_vector(3, column_sum(normed_grad))
            middle_grad = grad + norm_backward(normed_grad, hat, rho, vector(2))
            carry[rows, :] = middle_grad
            attended = middle_grad.astype(bf16)
            out_sum[...] += dot_tn(mixed[step, rows, :], attended)
            before_out = dot_nt(attended, weight_out()).astype(bf16)
            mixed_grad[rows, :] = before_out
            product = before_out.astype(f32) * mixed[step, rows, :].astype(f32)
            head = jnp.where(iota((HEADS, D), 1) // 64 == iota((HEADS, D), 0), 1.0, 0.0).astype(bf16)
            high = product.astype(bf16)
            centre = dot_nt(head, high) + dot_nt(head, (product - high.astype(f32)).astype(bf16))
            for unit in range(size // UNIT):
                centres[start // UNIT + unit] = centre[:, unit * UNIT : (unit + 1) * UNIT]

        over_rows(query_rows(step), SIZES_BACK, body)

    def attend_back(step):
        inside = iota((SEQ, 1), 0) < length

        def each_pair(pair, carried):
            def lanes(offset):
                return pl.ds(pl.multiple_of(offset + pair * PAIR, PAIR), PAIR)

            def clear(start, size):
                projected_grad[at_rows(start, size), lanes(0)] = jnp.zeros((size, PAIR), bf16)

            key_sum[...] = jnp.zeros_like(key_sum)
            value_sum[...] = jnp.zeros_like(value_sum)
            own_keys = projected[step, :, lanes(D)]
            turned[...] = jnp.where(inside, own_keys, jnp.zeros_like(own_keys)).T

            def body(start, size):
                rows = at_rows(start, size)
                keys, values = projected[step, :, lanes(D)], projected[step, :, lanes(2 * D)]
                queries, grads = projected[step, rows, lanes(0)], mixed_grad[rows, lanes(0)]
                query_half = [jnp.where(o, queries, jnp.zeros_like(queries)) for o in own]
                grad_half = [jnp.where(o, grads, jnp.zeros_like(grads)) for o in own]
                weights, slopes = [], []
                for h in range(2):
                    units = [start // UNIT + unit for unit in range(size // UNIT)]
                    log = jnp.concatenate([logs[step, unit, pl.ds(2 * pair + h, 1), :] for unit in units], axis=1)
                    centre = jnp.concatenate([centres[unit, pl.ds(2 * pair + h, 1), :] for unit in units], axis=1)
                    attention = jnp.exp2(dot_nt(keys, query_half[h]) * SCORE_LOG2 - log)
                    slope = (attention * (dot_nt(values, grad_half[h]) - centre)).astype(bf16)
                    weights.append(attention.astype(bf16))
                    slopes.append(slope)
                value_sum[...] += dot(jnp.concatenate(weights, axis=1), jnp.concatenate(grad_half, axis=0))
                key_sum[...] += dot(jnp.concatenate(slopes, axis=1), jnp.concatenate(query_half, axis=0))
                turned_grads = [dot(turned[64 * h : 64 * (h + 1), :], slopes[h]) for h in range(2)]
                projected_grad[rows, lanes(0)] = (jnp.concatenate(turned_grads, axis=0).T * SCORE_SCALE).astype(bf16)

            covered = over_rows(query_rows(step), SIZES_ATTEND_BACK, body)
            rest_rows(covered, clear)
            projected_grad[:, lanes(D)] = jnp.where(inside, key_sum[...] * SCORE_SCALE, 0.0).astype(bf16)
            projected_grad[:, lanes(2 * D)] = jnp.where(inside, value_sum[...], 0.0).astype(bf16)
            return carried

        lax.fori_loop(0, PAIRS, each_pair, 0)

    def project_back(step):
        def body(start, size):
            rows = at_rows(start, size)
            hat, rho = normalize(state[step, rows, :])
            normed_low = (hat * vector(0) + vector(1)).astype(bf16)
            normed_grad = jnp.zeros((size, D), f32)
            for j in range(3):
                grads = projected_grad[rows, D * j : D * (j + 1)]
                qkv_sum[j] += dot_tn(normed_low, grads)
                normed_grad = normed_grad + dot_nt(grads, weight_qkv(j))
            add_vector(0, column_sum(normed_grad * hat))
            add_vector(1, column_sum(normed_grad))
            through = norm_backward(normed_grad, hat, rho, vector(0))
            direct = jnp.where(step == 1, state[2, rows, :], 0.0)
            carry[rows, :] = jnp.where(row_index(start, size) < length, carry[rows, :] + through + direct, 0.0)

        over_rows(length, SIZES_LENGTH, body)

    def backward(back_step, carried):
        step = 1 - back_step

        @pl.when(step == 0)
        def _():
            fetch().wait()

        feed_back(step)

        @pl.when(step == 1)
        def _():
            fetch().start()

        attend_back(step)
        project_back(step)
        return carried

    lax.fori_loop(0, 2, backward, 0)

    def place(row, rows, value):
        while rows:
            chunk, inside = divmod(row, CHUNK)
            some = min(rows, CHUNK - inside)
            at = PACKED * chunk + inside
            hidden[at : at + some, :] = value[:some]
            value, row, rows = value[some:], row + some, rows - some

    for j in range(3):
        for n in range(8):
            place(CHUNK * n + 64 * j, 64, qkv_sum[j, 64 * n : 64 * (n + 1), :].astype(bf16))
    place(1536, 512, out_sum[...].astype(bf16))
    for j in range(4):
        for at, rows, first in UP_SEGMENTS:
            place(2048 + at + rows * j, rows, up_sum[j, first : first + rows, :].astype(bf16))
        place(4096 + D * j, D, down_sum[j].T.astype(bf16))
    for n in range(DEVICES):
        extra = next_rows(n, qkv_sum, out_sum, up_sum, hidden, vector_sum).astype(bf16)
        hidden[PACKED * n + CHUNK : PACKED * (n + 1), :] = extra
    copies = []
    for dc in range(2):
        part_a, part_b = (keep_a, keep_b) if dc == 0 else (send_a, send_b)
        for plane, (dy, dx) in enumerate(PLANE):
            for dz in range(4):
                row = pl.multiple_of(chunk_of(meta, dy, dc, dz, dx) * PACKED, 16)
                for part, index, first, some in (
                    (part_a, 4 * dz + plane, 0, ROWS_A),
                    (part_b, 4 * plane + dz, ROWS_A, ROWS_B),
                ):
                    copy = pltpu.make_async_copy(
                        hidden.at[pl.ds(row + first, some), :], part.at[index], out_sem.at[len(copies)]
                    )
                    copy.start()
                    copies.append(copy)
    for copy in copies:
        copy.wait()


def layer(meta, states, cotangent, pieces):
    in_place = pl.BlockSpec(memory_space=pltpu.VMEM)
    outside = pl.BlockSpec(memory_space=pl.ANY)
    outputs = pl.pallas_call(
        layer_kernel,
        out_shape=(
            shape_of(SEQ, D),
            shape_of(SEQ, D),
            shape_of(16, ROWS_A, D, dtype=bf16),
            shape_of(16, ROWS_A, D, dtype=bf16),
            shape_of(16, ROWS_B, D, dtype=bf16),
            shape_of(16, ROWS_B, D, dtype=bf16),
            shape_of(8 * SEQ, D, dtype=bf16),
        ),
        in_specs=[pl.BlockSpec(memory_space=pltpu.SMEM)] + [in_place] * 2 + [outside] * 16,
        out_specs=(in_place, in_place) + (outside,) * 5,
        scratch_shapes=[
            pltpu.VMEM((DEVICES * CHUNK, D), bf16),
            pltpu.VMEM((DEVICES, EXTRA, D), bf16),
            pltpu.VMEM((EXTRA, D), f32),
            pltpu.VMEM((3, SEQ, D), f32),
            pltpu.VMEM((2, SEQ, 3 * D), bf16),
            pltpu.VMEM((2, SEQ, D), bf16),
            pltpu.VMEM((2, SEQ, D), f32),
            pltpu.VMEM((8 * SEQ, D), bf16),
            pltpu.VMEM((SEQ, D), bf16),
            pltpu.VMEM((SEQ, 3 * D), bf16),
            pltpu.VMEM((2, SEQ // UNIT, HEADS, UNIT), f32),
            pltpu.VMEM((SEQ // UNIT, HEADS, UNIT), f32),
            pltpu.VMEM((3, D, D), f32),
            pltpu.VMEM((D, D), f32),
            pltpu.VMEM((4, D, D), f32),
            pltpu.VMEM((4, D, D), f32),
            pltpu.VMEM((16, D), f32),
            pltpu.VMEM((8, D), f32),
            pltpu.VMEM((8, PAIR), f32),
            pltpu.VMEM((SEQ, PAIR), f32),
            pltpu.VMEM((SEQ, PAIR), f32),
            pltpu.VMEM((PAIR, SEQ), bf16),
            pltpu.SemaphoreType.DMA((96,)),
            pltpu.SemaphoreType.DMA,
            pltpu.SemaphoreType.DMA((64,)),
        ],
        compiler_params=pltpu.CompilerParams(vmem_limit_bytes=63 * 1024 * 1024),
        name="layer",
    )(meta, states, cotangent, *pieces)
    return outputs[0], outputs[1], outputs[2:6]


def to_chunks(flat):
    wide = flat[:QKV_END].reshape(8, 64, 3, D).transpose(0, 2, 1, 3).reshape(1536, D)
    up = flat[OUT_END:UP_END].reshape(512, 4, D)
    pieces = [up[first : first + rows].transpose(1, 0, 2).reshape(4 * rows, D) for _, rows, first in UP_SEGMENTS]
    return jnp.concatenate(
        [wide, flat[QKV_END:OUT_END].reshape(D, D), *pieces, flat[UP_END:DOWN_END].reshape(FF, D)], axis=0
    )


def from_chunks(rows):
    wide = rows[:1536].reshape(8, 3, 64, D).transpose(0, 2, 1, 3).reshape(-1)
    up = rows[2048:4096]
    pieces = [
        up[at : at + 4 * rows].reshape(4, rows, D).transpose(1, 0, 2).reshape(-1) for at, rows, _ in UP_SEGMENTS
    ]
    return jnp.concatenate([wide, rows[1536:2048].reshape(-1), *pieces, rows[4096:].reshape(-1)])


def row_tables():
    order = np.concatenate(
        [
            (np.arange(1536).reshape(8, 64, 3).transpose(0, 2, 1)).reshape(-1),
            np.arange(1536, 2048),
            *[
                2048 + 4 * first + np.arange(4 * rows).reshape(rows, 4).transpose(1, 0).reshape(-1)
                for _, rows, first in UP_SEGMENTS
            ],
            np.arange(4096, 6144),
        ]
    )
    source = np.full((DEVICES, CHUNK + EXTRA), -1, np.int32)
    target = np.tile(np.arange(CHUNK + EXTRA, dtype=np.int32), (DEVICES, 1))
    for n in range(DEVICES):
        source[n, :CHUNK] = order[CHUNK * n : CHUNK * (n + 1)] - CHUNK * n
        target[n, source[n, :CHUNK]] = np.arange(CHUNK)
        width = 3 if n + 1 < 8 else 4 if 11 <= n + 1 < 22 else 1
        for row in range(10):
            at = row if width == 1 else 4 * (row % width) + row // width
            source[n, CHUNK + at] = CHUNK + row
    return source, target


def pick_rows(table, device, rows, precision=None):
    wanted = lax.dynamic_slice(jnp.asarray(table), (device, 0), (1, CHUNK + EXTRA)).reshape(-1, 1)
    pick = (wanted == iota((CHUNK + EXTRA, CHUNK + EXTRA), 1)).astype(rows.dtype)
    return jnp.dot(pick, rows, precision=precision, preferred_element_type=f32)


def send(array, dy=0, dx=0, dz=0, dc=0):
    pairs = []
    for y in range(2):
        for c in range(2):
            for z in range(4):
                for x in range(2):
                    other = (((y ^ dy) * 2 + (c ^ dc)) * 4 + (z ^ dz)) * 2 + (x ^ dx)
                    pairs.append((((y * 2 + c) * 4 + z) * 2 + x, other))
    return lax.ppermute(array, ("dp", "fsdp"), pairs)


def gather_weights(params, device, meanwhile):
    source, _ = row_tables()
    shift = (NPARAM // DEVICES - CHUNK * D) * device
    edge = jnp.zeros((EXTRA * D,), bf16)
    line = jnp.concatenate([edge, params.astype(bf16), edge])
    rows = lax.dynamic_slice(line, (EXTRA * D - shift,), ((CHUNK + EXTRA) * D,)).reshape(CHUNK + EXTRA, D)
    rows = pick_rows(source, device, rows).astype(bf16)
    own_a, own_b = rows[:ROWS_A], rows[ROWS_A:]
    first_a = jnp.stack([own_a] + [send(own_a, dy, dx) for dy, dx in PLANE[1:]])
    first_b = jnp.stack([own_b] + [send(own_b, dz=dz) for dz in (1, 2, 3)])
    first_a, first_b, meanwhile = lax.optimization_barrier((first_a, first_b, meanwhile))
    all_b = [first_b] + [send(first_b, dy, dx) for dy, dx in PLANE[1:]]
    all_a = [first_a] + [send(first_a, dz=dz) for dz in (1, 2, 3)]
    other_a = [send(part, dc=1) for part in all_a]
    other_b = [send(part, dc=1) for part in all_b]
    return all_a + other_a + all_b + other_b, meanwhile


def cut_weights(flat):
    chunks = to_chunks(flat[:DOWN_END]).reshape(DEVICES, CHUNK, D)
    extra = jnp.zeros((DEVICES, EXTRA, D), bf16).at[DEVICES - 1, :10].set(flat[DOWN_END:].reshape(10, D))
    chunks = jnp.concatenate([chunks, extra], axis=1).reshape(2, 2, 4, 2, PACKED, D)
    parts_a = chunks[..., :ROWS_A, :].transpose(1, 2, 3, 0, 4, 5).reshape(8, 4, ROWS_A, D)
    parts_b = chunks[..., ROWS_A:, :].transpose(1, 3, 0, 2, 4, 5).reshape(8, 4, ROWS_B, D)
    return [parts_a[n] for n in range(8)] + [parts_b[n] for n in range(8)]


def reduce_grads(parts, device, place, final_states, input_grad):
    keep_a, send_a, keep_b, send_b = parts
    _, target = row_tables()
    core_b, core_a = send(send_b, dc=1), send(send_a, dc=1)
    final_states = restore(place, final_states, "restore_final")
    core_a, final_states = lax.optimization_barrier((core_a, final_states))
    pair_a = [keep_a[4 * n : 4 * n + 4] + core_a[4 * n : 4 * n + 4] for n in range(4)]
    pair_b = [keep_b[4 * n : 4 * n + 4] + core_b[4 * n : 4 * n + 4] for n in range(4)]
    got_a = [send(pair_a[dz], dz=dz) for dz in (1, 2, 3)]
    got_b = [send(pair_b[n], *PLANE[n]) for n in (1, 2, 3)]
    line_a = sum((part.astype(f32) for part in got_a), pair_a[0].astype(f32))
    plane_b = sum((part.astype(f32) for part in got_b), pair_b[0].astype(f32))
    line_a, plane_b, input_grad = lax.optimization_barrier((line_a, plane_b, input_grad))
    got_b = [send(plane_b[dz].astype(bf16), dz=dz) for dz in (1, 2, 3)]
    got_a = [send(line_a[n].astype(bf16), *PLANE[n]) for n in (1, 2, 3)]
    input_grad = restore(place, input_grad, "restore_grad")
    got_a, got_b, input_grad = lax.optimization_barrier((got_a, got_b, input_grad))
    own_a = sum((part.astype(f32) for part in got_a), line_a[0])
    own_b = sum((part.astype(f32) for part in got_b), plane_b[0])
    rows = pick_rows(target, device, jnp.concatenate([own_a, own_b], axis=0), lax.Precision.HIGHEST)
    shift = (NPARAM // DEVICES - CHUNK * D) * device
    return lax.dynamic_slice(rows.reshape(-1), (shift,), (NPARAM // DEVICES,)), final_states, input_grad


def sum_all(value):
    value = jnp.broadcast_to(value, (8, 128))
    value = value + send(value, dc=1)
    value = value + sum(send(value, dy, dx) for dy, dx in PLANE[1:])
    return (value + sum(send(value, dz=dz) for dz in (1, 2, 3)))[0, 0]


def flat_grads(parts):
    keep_a, send_a, keep_b, send_b = parts
    chunks_a = jnp.stack([keep_a, send_a]).reshape(2, 4, 2, 2, ROWS_A, D).transpose(3, 0, 1, 2, 4, 5)
    chunks_b = jnp.stack([keep_b, send_b]).reshape(2, 2, 2, 4, ROWS_B, D).transpose(2, 0, 3, 1, 4, 5)
    chunks = jnp.concatenate(
        [chunks_a.reshape(DEVICES, ROWS_A, D), chunks_b.reshape(DEVICES, ROWS_B, D)], axis=1
    )
    rows = chunks[:, :CHUNK].reshape(DEVICES * CHUNK, D)
    vectors = chunks[DEVICES - 1, CHUNK : CHUNK + 10].reshape(-1)
    return jnp.concatenate([from_chunks(rows), vectors]).astype(f32)


def local(ways, states, params, first_moment, second_moment, ema_params, lengths, halt_counts, cotangent):
    both = ("dp", "fsdp")
    device = lax.axis_index(both)
    blockwise = ways == (4, 8)
    if blockwise:
        outer, inner = lax.axis_index("dp"), lax.axis_index("fsdp")
        place_index = jnp.stack([outer // 2, outer % 2, inner // 2, inner % 2]).astype(i32)
    else:
        place_index = jnp.zeros((4,), i32)
    prepared = prepare(lengths, place_index, halt_counts, states[0], cotangent[0])
    if blockwise:
        pieces, prepared = gather_weights(params, device, prepared)
    else:
        pieces = cut_weights(lax.all_gather(params.astype(bf16), both, axis=0, tiled=True))
    place, sorted_states, sorted_cotangent, meta = prepared
    final_states, input_grad, parts = layer(meta, sorted_states, sorted_cotangent, pieces)
    if blockwise:
        reduced, final_states, input_grad = reduce_grads(parts, device, place, final_states, input_grad)
        square_sum = sum_all(jnp.sum(reduced * reduced))
    else:
        final_states = restore(place, final_states, "restore_final")
        input_grad = restore(place, input_grad, "restore_grad")
        reduced = lax.psum_scatter(flat_grads(parts), both, scatter_dimension=0, tiled=True)
        square_sum = lax.psum(jnp.sum(reduced * reduced), both)
    grad_norm = jnp.sqrt(square_sum)
    clip_bound = NPARAM**0.5
    clipped = reduced * (clip_bound / jnp.maximum(grad_norm, clip_bound))
    new_first = BETA_FIRST * first_moment + (1.0 - BETA_FIRST) * clipped
    new_second = BETA_SECOND * second_moment + (1.0 - BETA_SECOND) * clipped * clipped
    first_hat = new_first / (1.0 - BETA_FIRST**ADAM_STEP)
    second_hat = new_second / (1.0 - BETA_SECOND**ADAM_STEP)
    shard_length = params.shape[0]
    index_all = device * shard_length + iota((shard_length,), 0)
    matrix = index_all < DOWN_END
    step_rate = jnp.where(matrix, RATE_MATRIX, RATE_VECTOR)
    decay_rate = jnp.where(matrix, WEIGHT_DECAY, 0.0)
    new_params = params - step_rate * (first_hat / (jnp.sqrt(second_hat) + ADAM_EPSILON) + decay_rate * params)
    average_decay = min(EMA_DECAY, (1.0 + ADAM_STEP) / (10.0 + ADAM_STEP))
    new_ema = average_decay * ema_params + (1.0 - average_decay) * new_params
    return (
        final_states[None],
        input_grad[None],
        clipped,
        grad_norm.reshape(1),
        new_params,
        new_first,
        new_second,
        new_ema,
        new_params.astype(bf16),
    )


def solution(mesh):
    both = ("dp", "fsdp")
    wide, flat, counts = P(both, None, None), P(both), P(both, None)
    ways = (mesh.shape["dp"], mesh.shape["fsdp"])
    return jax.shard_map(
        functools.partial(local, ways),
        mesh=mesh,
        in_specs=(wide, flat, flat, flat, flat, flat, counts, wide),
        out_specs=(wide, wide, flat, P(), flat, flat, flat, flat, flat),
        check_vma=False,
    )
```

profile of v0, /device:TPU:0, one launch (start us, length us, event | category | flops | bytes accessed | tf_op | source)
XLA Modules:
  0.0 274.8 jit_solution(17322977625518302471)
XLA Ops:
  0.7 1.0 convert_element_type.77
  1.7 1.3 concatenate.6
  4.3 3.0 %collective-permute-start.1 = (bf16[64,512]{1,0:T(8,128)(2,1)S(1)}, bf16[64,512]{1,0:T(8,128)(2,1)S(1)}, u32[]{:S(2)}, u32[]{:S(2)}) collective-permute-start(bf16[64,512]{1,0:T(8,128)(2,1)S(1)} %get-tuple-element.85), channel_id=1, source_target_pairs={{0,1},{1,0},{2,3},{3,2},{4,5},{5,4},{6,7},{7,6},{8,9},{9,8},{10,11... | collective-permute-start | bytes 196616 | tf_op jit(solution)/shard_map/ppermute | solution.py:736
  7.3 1.5 collective-permute-start
  8.9 3.1 %collective-permute-start.4 = (bf16[144,512]{1,0:T(8,128)(2,1)S(1)}, bf16[144,512]{1,0:T(8,128)(2,1)S(1)}, u32[]{:S(2)}, u32[]{:S(2)}) collective-permute-start(bf16[144,512]{1,0:T(8,128)(2,1)S(1)} %get-tuple-element.83), channel_id=1, source_target_pairs={{0,4},{1,5},{2,6},{3,7},{4,0},{5,1},{6,2},{7,3},{8,12},{9,13},{10,... | collective-permute-start | bytes 442376 | tf_op jit(solution)/shard_map/ppermute | solution.py:736
  12.0 1.6 collective-permute-start.3
  14.9 5.8 %prepare.1 = (f32[8,1024]{1,0:T(8,128)}, bf16[1024,512]{1,0:T(8,128)(2,1)}, bf16[1024,512]{1,0:T(8,128)(2,1)}, s32[6]{0:T(128)}) custom-call(s32[1]{0:T(128)S(6)} %copy.20.length_ref, s32[4]{0:T(128)} %pad_add_fusion.index_ref, s32[1,1024]{1,0:T(1,128)} %count_ref.1, bf16[1024,512]{1,0:T(8,128)(2,1)} %bitcast.60, bf16[1024,512]{1,0:T(8,128)(2,1)} %bitcast.61), custom_call_target="tpu_custom_call" | custom-call | flops 6000000000 | bytes 4000000 | tf_op jit(solution)/shard_map/prepare/pallas_call | solution.py:140
  20.7 1.8 collective-permute-done.4
  22.7 2.5 collective-permute-start.15
  26.3 2.9 %collective-permute-start.8 = (bf16[4,64,512]{2,1,0:T(8,128)(2,1)S(1)}, bf16[4,64,512]{2,1,0:T(8,128)(2,1)S(1)}, u32[]{:S(2)}, u32[]{:S(2)}) collective-permute-start(bf16[4,64,512]{2,1,0:T(8,128)(2,1)S(1)} %pad_maximum_fusion.1.refs_0_), channel_id=1, source_target_pairs={{0,6},{1,7},{2,4},{3,5},{4,2},{5,3},{6,0},{7,1},{8,14},{9,15},{10,... | collective-permute-start | bytes 786440 | tf_op jit(solution)/shard_map/ppermute | solution.py:736
  29.2 1.8 collective-permute-start.7
  30.9 6.5 %collective-permute-done.8.refs_3_ = bf16[4,64,512]{2,1,0:T(8,128)(2,1)S(1)} collective-permute-done((bf16[4,64,512]{2,1,0:T(8,128)(2,1)S(1)}, bf16[4,64,512]{2,1,0:T(8,128)(2,1)S(1)}, u32[]{:S(2)}, u32[]{:S(2)}) %collective-permute-start.8) | collective-permute-done | bytes 262176 | tf_op jit(solution)/shard_map/ppermute | solution.py:736
  37.4 10.4 %collective-permute-start.6 = (bf16[4,64,512]{2,1,0:T(8,128)(2,1)S(1)}, bf16[4,64,512]{2,1,0:T(8,128)(2,1)S(1)}, u32[]{:S(2)}, u32[]{:S(2)}) collective-permute-start(bf16[4,64,512]{2,1,0:T(8,128)(2,1)S(1)} %pad_maximum_fusion.1.refs_0_), channel_id=1, source_target_pairs={{0,2},{1,3},{2,0},{3,1},{4,6},{5,7},{6,4},{7,5},{8,10},{9,11},{10,... | collective-permute-start | bytes 786440 | tf_op jit(solution)/shard_map/ppermute | solution.py:736
  47.8 5.1 %collective-permute-done.7.refs_2_ = bf16[4,64,512]{2,1,0:T(8,128)(2,1)S(1)} collective-permute-done((bf16[4,64,512]{2,1,0:T(8,128)(2,1)S(1)}, bf16[4,64,512]{2,1,0:T(8,128)(2,1)S(1)}, u32[]{:S(2)}, u32[]{:S(2)}) %collective-permute-start.7) | collective-permute-done | bytes 262176 | tf_op jit(solution)/shard_map/ppermute | solution.py:736
  52.9 5.5 %collective-permute-done.6.refs_1_ = bf16[4,64,512]{2,1,0:T(8,128)(2,1)S(1)} collective-permute-done((bf16[4,64,512]{2,1,0:T(8,128)(2,1)S(1)}, bf16[4,64,512]{2,1,0:T(8,128)(2,1)S(1)}, u32[]{:S(2)}, u32[]{:S(2)}) %collective-permute-start.6) | collective-permute-done | bytes 262176 | tf_op jit(solution)/shard_map/ppermute | solution.py:736
  59.5 3.8 %collective-permute-done.11.refs_6_ = bf16[4,64,512]{2,1,0:T(8,128)(2,1)S(1)} collective-permute-done((bf16[4,64,512]{2,1,0:T(8,128)(2,1)S(1)}, bf16[4,64,512]{2,1,0:T(8,128)(2,1)S(1)}, u32[]{:S(2)}, u32[]{:S(2)}) %collective-permute-start.11) | collective-permute-done | bytes 262176 | tf_op jit(solution)/shard_map/ppermute | solution.py:736
  63.4 1.4 collective-permute-done.10.refs_5_
  66.8 108.3 %layer.1 = (f32[1024,512]{1,0:T(8,128)}, f32[1024,512]{1,0:T(8,128)}, bf16[16,64,512]{2,1,0:T(8,128)(2,1)}, bf16[16,64,512]{2,1,0:T(8,128)(2,1)}, bf16[16,144,51...) custom-call(s32[6]{0:T(128)} %get-tuple-element.41.meta, ...), custom_call_target="tpu_custom_call" | custom-call | tf_op jit(solution)/shard_map/layer/pallas_call | solution.py:634
  175.6 6.6 %restore_final.1 = f32[1024,512]{1,0:T(8,128)} custom-call(f32[8,1024]{1,0:T(8,128)} %get-tuple-element.47.place_ref, f32[1024,512]{1,0:T(8,128)} %get-tuple-element.48.sorted_ref), custom_call_target="tpu_custom_call" | custom-call | flops 6000000000 | bytes 4000000 | tf_op jit(solution)/shard_map/restore_final/pallas_call | solution.py:187
  182.2 2.1 slice_add_fusion.6
  184.4 1.5 slice_add_fusion.2
  186.3 10.3 %collective-permute-start.25 = (bf16[4,144,512]{2,1,0:T(8,128)(2,1)}, bf16[4,144,512]{2,1,0:T(8,128)(2,1)S(1)}, u32[]{:S(2)}, u32[]{:S(2)}) collective-permute-start(bf16[4,144,512]{2,1,0:T(8,128)(2,1)} %get-tuple-element.70), channel_id=1, source_target_pairs={{0,16},{1,17},{2,18},{3,19},{4,20},{5,21},{6,22},{7,23},{8,24},{9,... | collective-permute-start | bytes 1769480 | tf_op jit(solution)/shard_map/ppermute | solution.py:736
  196.6 3.7 %collective-permute-start.27 = (bf16[4,144,512]{2,1,0:T(8,128)(2,1)}, bf16[4,144,512]{2,1,0:T(8,128)(2,1)}, u32[]{:S(2)}, u32[]{:S(2)}) collective-permute-start(bf16[4,144,512]{2,1,0:T(8,128)(2,1)} %get-tuple-element.71), channel_id=1, source_target_pairs={{0,17},{1,16},{2,19},{3,18},{4,21},{5,20},{6,23},{7,22},{8,25},{9,... | collective-permute-start | bytes 1769480 | tf_op jit(solution)/shard_map/ppermute | solution.py:736
  200.8 3.6 %collective-permute-start.23 = (bf16[4,64,512]{2,1,0:T(8,128)(2,1)}, bf16[4,64,512]{2,1,0:T(8,128)(2,1)S(1)}, u32[]{:S(2)}, u32[]{:S(2)}) collective-permute-start(bf16[4,64,512]{2,1,0:T(8,128)(2,1)} %get-tuple-element.74), channel_id=1, source_target_pairs={{0,6},{1,7},{2,4},{3,5},{4,2},{5,3},{6,0},{7,1},{8,14},{9,15},{10,... | collective-permute-start | bytes 786440 | tf_op jit(solution)/shard_map/ppermute | solution.py:736
  204.5 1.9 collective-permute-start.22
  206.3 5.8 %collective-permute-done.23 = bf16[4,64,512]{2,1,0:T(8,128)(2,1)S(1)} collective-permute-done((bf16[4,64,512]{2,1,0:T(8,128)(2,1)}, bf16[4,64,512]{2,1,0:T(8,128)(2,1)S(1)}, u32[]{:S(2)}, u32[]{:S(2)}) %collective-permute-start.23) | collective-permute-done | bytes 262176 | tf_op jit(solution)/shard_map/ppermute | solution.py:736
  212.1 15.4 %collective-permute-done.22 = bf16[4,64,512]{2,1,0:T(8,128)(2,1)S(1)} collective-permute-done((bf16[4,64,512]{2,1,0:T(8,128)(2,1)}, bf16[4,64,512]{2,1,0:T(8,128)(2,1)S(1)}, u32[]{:S(2)}, u32[]{:S(2)}) %collective-permute-start.22) | collective-permute-done | bytes 262176 | tf_op jit(solution)/shard_map/ppermute | solution.py:736
  227.5 1.2 convert_add_fusion.1
  228.7 2.0 convert_add_fusion
  231.4 2.3 collective-permute-start.30
  235.0 2.7 collective-permute-start.33
  237.7 1.7 collective-permute-start.31
  239.5 6.5 %restore_grad.1 = f32[1024,512]{1,0:T(8,128)} custom-call(f32[8,1024]{1,0:T(8,128)} %get-tuple-element.47.place_ref, f32[1024,512]{1,0:T(8,128)} %get-tuple-element.57.sorted_ref), custom_call_target="tpu_custom_call" | custom-call | flops 6000000000 | bytes 4000000 | tf_op jit(solution)/shard_map/restore_grad/pallas_call | solution.py:187
  246.0 3.3 %collective-permute-done.32 = bf16[144,512]{1,0:T(8,128)(2,1)} collective-permute-done((bf16[144,512]{1,0:T(8,128)(2,1)S(1)}, bf16[144,512]{1,0:T(8,128)(2,1)}, u32[]{:S(2)}, u32[]{:S(2)}) %collective-permute-start.32) | collective-permute-done | bytes 147488 | tf_op jit(solution)/shard_map/ppermute | solution.py:736
  249.3 1.0 fusion.5
  250.3 0.9 fusion.7
  253.3 1.2 collective-permute-done.34
  255.1 2.2 collective-permute-start.37
  257.3 0.8 collective-permute-start.36
  258.7 1.0 collective-permute-done.37
  259.7 1.3 collective-permute-done.36
  260.9 0.8 collective-permute-done.35
  262.4 2.6 collective-permute-start.40
  265.0 1.9 collective-permute-start.38
  266.9 1.1 collective-permute-done.40
  267.9 1.6 collective-permute-done.39
  270.8 1.5 fusion.11
  272.3 0.9 multiply_add_fusion
  (116 shorter events, 14.3 us)
Async XLA Ops:
  4.3 10.5 %collective-permute-start.1 = (bf16[64,512]{1,0:T(8,128)(2,1)S(1)}, bf16[64,512]{1,0:T(8,128)(2,1)S(1)}, u32[]{:S(2)}, u32[]{:S(2)}) collective-permute-start(bf16[64,512]{1,0:T(8,128)(2,1)S(1)} %get-tuple-element.85), channel_id=1, source_target_pairs={{0,1},{1,0},{2,3},{3,2},{4,5},{5,4},{6,7},{7,6},{8,9},{9,8},{10,11... | collective-permute-start | bytes 196616 | tf_op jit(solution)/shard_map/ppermute | solution.py:736
  7.3 13.3 %collective-permute-start = (bf16[64,512]{1,0:T(8,128)(2,1)S(1)}, bf16[64,512]{1,0:T(8,128)(2,1)S(1)}, u32[]{:S(2)}, u32[]{:S(2)}) collective-permute-start(bf16[64,512]{1,0:T(8,128)(2,1)S(1)} %get-tuple-element.85), channel_id=1, source_target_pairs={{0,16},{1,17},{2,18},{3,19},{4,20},{5,21},{6,22},{7,23},{8,24},{9,... | collective-permute-start | bytes 196616 | tf_op jit(solution)/shard_map/ppermute | solution.py:736
  8.9 11.8 %collective-permute-start.2 = (bf16[64,512]{1,0:T(8,128)(2,1)S(1)}, bf16[64,512]{1,0:T(8,128)(2,1)S(1)}, u32[]{:S(2)}, u32[]{:S(2)}) collective-permute-start(bf16[64,512]{1,0:T(8,128)(2,1)S(1)} %get-tuple-element.85), channel_id=1, source_target_pairs={{0,17},{1,16},{2,19},{3,18},{4,21},{5,20},{6,23},{7,22},{8,25},{9,... | collective-permute-start | bytes 196616 | tf_op jit(solution)/shard_map/ppermute | solution.py:736
  8.9 13.7 %collective-permute-start.4 = (bf16[144,512]{1,0:T(8,128)(2,1)S(1)}, bf16[144,512]{1,0:T(8,128)(2,1)S(1)}, u32[]{:S(2)}, u32[]{:S(2)}) collective-permute-start(bf16[144,512]{1,0:T(8,128)(2,1)S(1)} %get-tuple-element.83), channel_id=1, source_target_pairs={{0,4},{1,5},{2,6},{3,7},{4,0},{5,1},{6,2},{7,3},{8,12},{9,13},{10,... | collective-permute-start | bytes 442376 | tf_op jit(solution)/shard_map/ppermute | solution.py:736
  12.0 10.6 %collective-permute-start.3 = (bf16[144,512]{1,0:T(8,128)(2,1)S(1)}, bf16[144,512]{1,0:T(8,128)(2,1)S(1)}, u32[]{:S(2)}, u32[]{:S(2)}) collective-permute-start(bf16[144,512]{1,0:T(8,128)(2,1)S(1)} %get-tuple-element.83), channel_id=1, source_target_pairs={{0,2},{1,3},{2,0},{3,1},{4,6},{5,7},{6,4},{7,5},{8,10},{9,11},{10,... | collective-permute-start | bytes 442376 | tf_op jit(solution)/shard_map/ppermute | solution.py:736
  14.9 7.7 %collective-permute-start.5 = (bf16[144,512]{1,0:T(8,128)(2,1)S(1)}, bf16[144,512]{1,0:T(8,128)(2,1)S(1)}, u32[]{:S(2)}, u32[]{:S(2)}) collective-permute-start(bf16[144,512]{1,0:T(8,128)(2,1)S(1)} %get-tuple-element.83), channel_id=1, source_target_pairs={{0,6},{1,7},{2,4},{3,5},{4,2},{5,3},{6,0},{7,1},{8,14},{9,15},{10,... | collective-permute-start | bytes 442376 | tf_op jit(solution)/shard_map/ppermute | solution.py:736
  20.7 46.0 %copy-start.5 = (bf16[4,64,512]{2,1,0:T(8,128)(2,1)}, bf16[4,64,512]{2,1,0:T(8,128)(2,1)S(1)}, u32[]{:S(2)}) copy-start(bf16[4,64,512]{2,1,0:T(8,128)(2,1)S(1)} %pad_maximum_fusion.1.refs_0_) | copy-start | bytes 786436
  22.7 44.1 %copy-start = (bf16[4,144,512]{2,1,0:T(8,128)(2,1)}, bf16[4,144,512]{2,1,0:T(8,128)(2,1)S(1)}, u32[]{:S(2)}) copy-start(bf16[4,144,512]{2,1,0:T(8,128)(2,1)S(1)} %pad_maximum_fusion.refs_8_) | copy-start | bytes 1769476
  22.7 6.5 %collective-permute-start.9 = (bf16[4,64,512]{2,1,0:T(8,128)(2,1)S(1)}, bf16[4,64,512]{2,1,0:T(8,128)(2,1)S(1)}, u32[]{:S(2)}, u32[]{:S(2)}) collective-permute-start(bf16[4,64,512]{2,1,0:T(8,128)(2,1)S(1)} %pad_maximum_fusion.1.refs_0_), channel_id=1, source_target_pairs={{0,8},{1,9},{2,10},{3,11},{4,12},{5,13},{6,14},{7,15},{8,0},{9,1},... | collective-permute-start | bytes 786440 | tf_op jit(solution)/shard_map/ppermute | solution.py:736
  22.7 35.7 %collective-permute-start.15 = (bf16[4,144,512]{2,1,0:T(8,128)(2,1)S(1)}, bf16[4,144,512]{2,1,0:T(8,128)(2,1)S(1)}, u32[]{:S(2)}, u32[]{:S(2)}) collective-permute-start(bf16[4,144,512]{2,1,0:T(8,128)(2,1)S(1)} %pad_maximum_fusion.refs_8_), channel_id=1, source_target_pairs={{0,17},{1,16},{2,19},{3,18},{4,21},{5,20},{6,23},{7,22},{8,25},{9,... | collective-permute-start | bytes 1769480 | tf_op jit(solution)/shard_map/ppermute | solution.py:736
  25.3 33.6 %collective-permute-start.14 = (bf16[4,144,512]{2,1,0:T(8,128)(2,1)S(1)}, bf16[4,144,512]{2,1,0:T(8,128)(2,1)S(1)}, u32[]{:S(2)}, u32[]{:S(2)}) collective-permute-start(bf16[4,144,512]{2,1,0:T(8,128)(2,1)S(1)} %pad_maximum_fusion.refs_8_), channel_id=1, source_target_pairs={{0,1},{1,0},{2,3},{3,2},{4,5},{5,4},{6,7},{7,6},{8,9},{9,8},{10,11... | collective-permute-start | bytes 1769480 | tf_op jit(solution)/shard_map/ppermute | solution.py:736
  25.8 33.2 %collective-permute-start.13 = (bf16[4,144,512]{2,1,0:T(8,128)(2,1)S(1)}, bf16[4,144,512]{2,1,0:T(8,128)(2,1)S(1)}, u32[]{:S(2)}, u32[]{:S(2)}) collective-permute-start(bf16[4,144,512]{2,1,0:T(8,128)(2,1)S(1)} %pad_maximum_fusion.refs_8_), channel_id=1, source_target_pairs={{0,16},{1,17},{2,18},{3,19},{4,20},{5,21},{6,22},{7,23},{8,24},{9,... | collective-permute-start | bytes 1769480 | tf_op jit(solution)/shard_map/ppermute | solution.py:736
  26.3 11.1 %collective-permute-start.8 = (bf16[4,64,512]{2,1,0:T(8,128)(2,1)S(1)}, bf16[4,64,512]{2,1,0:T(8,128)(2,1)S(1)}, u32[]{:S(2)}, u32[]{:S(2)}) collective-permute-start(bf16[4,64,512]{2,1,0:T(8,128)(2,1)S(1)} %pad_maximum_fusion.1.refs_0_), channel_id=1, source_target_pairs={{0,6},{1,7},{2,4},{3,5},{4,2},{5,3},{6,0},{7,1},{8,14},{9,15},{10,... | collective-permute-start | bytes 786440 | tf_op jit(solution)/shard_map/ppermute | solution.py:736
  29.2 23.7 %copy-start.16 = (bf16[4,64,512]{2,1,0:T(8,128)(2,1)}, bf16[4,64,512]{2,1,0:T(8,128)(2,1)S(1)}, u32[]{:S(2)}) copy-start(bf16[4,64,512]{2,1,0:T(8,128)(2,1)S(1)} %collective-permute-done.9.refs_4_) | copy-start | bytes 786436
  29.2 23.7 %collective-permute-start.7 = (bf16[4,64,512]{2,1,0:T(8,128)(2,1)S(1)}, bf16[4,64,512]{2,1,0:T(8,128)(2,1)S(1)}, u32[]{:S(2)}, u32[]{:S(2)}) collective-permute-start(bf16[4,64,512]{2,1,0:T(8,128)(2,1)S(1)} %pad_maximum_fusion.1.refs_0_), channel_id=1, source_target_pairs={{0,4},{1,5},{2,6},{3,7},{4,0},{5,1},{6,2},{7,3},{8,12},{9,13},{10,... | collective-permute-start | bytes 786440 | tf_op jit(solution)/shard_map/ppermute | solution.py:736
  37.4 27.5 %copy-start.17 = (bf16[4,64,512]{2,1,0:T(8,128)(2,1)}, bf16[4,64,512]{2,1,0:T(8,128)(2,1)S(1)}, u32[]{:S(2)}) copy-start(bf16[4,64,512]{2,1,0:T(8,128)(2,1)S(1)} %collective-permute-done.8.refs_3_) | copy-start | bytes 786436
  37.4 21.0 %collective-permute-start.6 = (bf16[4,64,512]{2,1,0:T(8,128)(2,1)S(1)}, bf16[4,64,512]{2,1,0:T(8,128)(2,1)S(1)}, u32[]{:S(2)}, u32[]{:S(2)}) collective-permute-start(bf16[4,64,512]{2,1,0:T(8,128)(2,1)S(1)} %pad_maximum_fusion.1.refs_0_), channel_id=1, source_target_pairs={{0,2},{1,3},{2,0},{3,1},{4,6},{5,7},{6,4},{7,5},{8,10},{9,11},{10,... | collective-permute-start | bytes 786440 | tf_op jit(solution)/shard_map/ppermute | solution.py:736
  52.9 6.6 %collective-permute-start.12 = (bf16[4,64,512]{2,1,0:T(8,128)(2,1)S(1)}, bf16[4,64,512]{2,1,0:T(8,128)(2,1)S(1)}, u32[]{:S(2)}, u32[]{:S(2)}) collective-permute-start(bf16[4,64,512]{2,1,0:T(8,128)(2,1)S(1)} %collective-permute-done.8.refs_3_), channel_id=1, source_target_pairs={{0,8},{1,9},{2,10},{3,11},{4,12},{5,13},{6,14},{7,15},{8,0},{9,1},... | collective-permute-start | bytes 786440 | tf_op jit(solution)/shard_map/ppermute | solution.py:736
  58.4 6.5 %collective-permute-start.16 = (bf16[4,144,512]{2,1,0:T(8,128)(2,1)S(1)}, bf16[4,144,512]{2,1,0:T(8,128)(2,1)S(1)}, u32[]{:S(2)}, u32[]{:S(2)}) collective-permute-start(bf16[4,144,512]{2,1,0:T(8,128)(2,1)S(1)} %pad_maximum_fusion.refs_8_), channel_id=1, source_target_pairs={{0,8},{1,9},{2,10},{3,11},{4,12},{5,13},{6,14},{7,15},{8,0},{9,1},... | collective-permute-start | bytes 1769480 | tf_op jit(solution)/shard_map/ppermute | solution.py:736
  58.4 6.4 %collective-permute-start.19 = (bf16[4,144,512]{2,1,0:T(8,128)(2,1)S(1)}, bf16[4,144,512]{2,1,0:T(8,128)(2,1)S(1)}, u32[]{:S(2)}, u32[]{:S(2)}) collective-permute-start(bf16[4,144,512]{2,1,0:T(8,128)(2,1)S(1)} %collective-permute-done.15.refs_11_), channel_id=1, source_target_pairs={{0,8},{1,9},{2,10},{3,11},{4,12},{5,13},{6,14},{7,15},{8,0},{9,1},... | collective-permute-start | bytes 1769480 | tf_op jit(solution)/shard_map/ppermute | solution.py:736
  58.9 6.0 %collective-permute-start.18 = (bf16[4,144,512]{2,1,0:T(8,128)(2,1)S(1)}, bf16[4,144,512]{2,1,0:T(8,128)(2,1)S(1)}, u32[]{:S(2)}, u32[]{:S(2)}) collective-permute-start(bf16[4,144,512]{2,1,0:T(8,128)(2,1)S(1)} %collective-permute-done.14.refs_10_), channel_id=1, source_target_pairs={{0,8},{1,9},{2,10},{3,11},{4,12},{5,13},{6,14},{7,15},{8,0},{9,1},... | collective-permute-start | bytes 1769480 | tf_op jit(solution)/shard_map/ppermute | solution.py:736
  59.0 7.8 %collective-permute-start.17 = (bf16[4,144,512]{2,1,0:T(8,128)(2,1)S(1)}, bf16[4,144,512]{2,1,0:T(8,128)(2,1)}, u32[]{:S(2)}, u32[]{:S(2)}) collective-permute-start(bf16[4,144,512]{2,1,0:T(8,128)(2,1)S(1)} %collective-permute-done.13.refs_9_), channel_id=1, source_target_pairs={{0,8},{1,9},{2,10},{3,11},{4,12},{5,13},{6,14},{7,15},{8,0},{9,1},... | collective-permute-start | bytes 1769480 | tf_op jit(solution)/shard_map/ppermute | solution.py:736
  59.4 3.9 %collective-permute-start.11 = (bf16[4,64,512]{2,1,0:T(8,128)(2,1)S(1)}, bf16[4,64,512]{2,1,0:T(8,128)(2,1)S(1)}, u32[]{:S(2)}, u32[]{:S(2)}) collective-permute-start(bf16[4,64,512]{2,1,0:T(8,128)(2,1)S(1)} %collective-permute-done.7.refs_2_), channel_id=1, source_target_pairs={{0,8},{1,9},{2,10},{3,11},{4,12},{5,13},{6,14},{7,15},{8,0},{9,1},... | collective-permute-start | bytes 786440 | tf_op jit(solution)/shard_map/ppermute | solution.py:736
  63.3 1.5 collective-permute-start.10
  175.0 9.3 %collective-permute-start.24 = (bf16[16,144,512]{2,1,0:T(8,128)(2,1)}, bf16[16,144,512]{2,1,0:T(8,128)(2,1)S(1)}, u32[]{:S(2)}, u32[]{:S(2)}) collective-permute-start(bf16[16,144,512]{2,1,0:T(8,128)(2,1)} %get-tuple-element.53), channel_id=1, source_target_pairs={{0,8},{1,9},{2,10},{3,11},{4,12},{5,13},{6,14},{7,15},{8,0},{9,1},... | collective-permute-start | bytes 7077896 | tf_op jit(solution)/shard_map/ppermute | solution.py:736
  175.1 7.1 %collective-permute-start.20 = (bf16[16,64,512]{2,1,0:T(8,128)(2,1)}, bf16[16,64,512]{2,1,0:T(8,128)(2,1)}, u32[]{:S(2)}, u32[]{:S(2)}) collective-permute-start(bf16[16,64,512]{2,1,0:T(8,128)(2,1)} %get-tuple-element.46), channel_id=1, source_target_pairs={{0,8},{1,9},{2,10},{3,11},{4,12},{5,13},{6,14},{7,15},{8,0},{9,1},... | collective-permute-start | bytes 3145736 | tf_op jit(solution)/shard_map/ppermute | solution.py:736
  184.3 20.1 %collective-permute-start.21 = (bf16[4,64,512]{2,1,0:T(8,128)(2,1)S(1)}, bf16[4,64,512]{2,1,0:T(8,128)(2,1)}, u32[]{:S(2)}, u32[]{:S(2)}) collective-permute-start(bf16[4,64,512]{2,1,0:T(8,128)(2,1)S(1)} %get-tuple-element.73), channel_id=1, source_target_pairs={{0,2},{1,3},{2,0},{3,1},{4,6},{5,7},{6,4},{7,5},{8,10},{9,11},{10,... | collective-permute-start | bytes 786440 | tf_op jit(solution)/shard_map/ppermute | solution.py:736
  186.3 42.4 %collective-permute-start.25 = (bf16[4,144,512]{2,1,0:T(8,128)(2,1)}, bf16[4,144,512]{2,1,0:T(8,128)(2,1)S(1)}, u32[]{:S(2)}, u32[]{:S(2)}) collective-permute-start(bf16[4,144,512]{2,1,0:T(8,128)(2,1)} %get-tuple-element.70), channel_id=1, source_target_pairs={{0,16},{1,17},{2,18},{3,19},{4,20},{5,21},{6,22},{7,23},{8,24},{9,... | collective-permute-start | bytes 1769480 | tf_op jit(solution)/shard_map/ppermute | solution.py:736
  196.6 32.1 %collective-permute-start.27 = (bf16[4,144,512]{2,1,0:T(8,128)(2,1)}, bf16[4,144,512]{2,1,0:T(8,128)(2,1)}, u32[]{:S(2)}, u32[]{:S(2)}) collective-permute-start(bf16[4,144,512]{2,1,0:T(8,128)(2,1)} %get-tuple-element.71), channel_id=1, source_target_pairs={{0,17},{1,16},{2,19},{3,18},{4,21},{5,20},{6,23},{7,22},{8,25},{9,... | collective-permute-start | bytes 1769480 | tf_op jit(solution)/shard_map/ppermute | solution.py:736
  200.3 28.5 %collective-permute-start.26 = (bf16[4,144,512]{2,1,0:T(8,128)(2,1)}, bf16[4,144,512]{2,1,0:T(8,128)(2,1)}, u32[]{:S(2)}, u32[]{:S(2)}) collective-permute-start(bf16[4,144,512]{2,1,0:T(8,128)(2,1)} %get-tuple-element.72), channel_id=1, source_target_pairs={{0,1},{1,0},{2,3},{3,2},{4,5},{5,4},{6,7},{7,6},{8,9},{9,8},{10,11... | collective-permute-start | bytes 1769480 | tf_op jit(solution)/shard_map/ppermute | solution.py:736
  200.8 11.3 %collective-permute-start.23 = (bf16[4,64,512]{2,1,0:T(8,128)(2,1)}, bf16[4,64,512]{2,1,0:T(8,128)(2,1)S(1)}, u32[]{:S(2)}, u32[]{:S(2)}) collective-permute-start(bf16[4,64,512]{2,1,0:T(8,128)(2,1)} %get-tuple-element.74), channel_id=1, source_target_pairs={{0,6},{1,7},{2,4},{3,5},{4,2},{5,3},{6,0},{7,1},{8,14},{9,15},{10,... | collective-permute-start | bytes 786440 | tf_op jit(solution)/shard_map/ppermute | solution.py:736
  204.5 23.0 %collective-permute-start.22 = (bf16[4,64,512]{2,1,0:T(8,128)(2,1)}, bf16[4,64,512]{2,1,0:T(8,128)(2,1)S(1)}, u32[]{:S(2)}, u32[]{:S(2)}) collective-permute-start(bf16[4,64,512]{2,1,0:T(8,128)(2,1)} %get-tuple-element.75), channel_id=1, source_target_pairs={{0,4},{1,5},{2,6},{3,7},{4,0},{5,1},{6,2},{7,3},{8,12},{9,13},{10,... | collective-permute-start | bytes 786440 | tf_op jit(solution)/shard_map/ppermute | solution.py:736
  231.4 6.3 %collective-permute-start.30 = (bf16[64,512]{1,0:T(8,128)(2,1)S(1)}, bf16[64,512]{1,0:T(8,128)(2,1)S(1)}, u32[]{:S(2)}, u32[]{:S(2)}) collective-permute-start(bf16[64,512]{1,0:T(8,128)(2,1)S(1)} %get-tuple-element.79), channel_id=1, source_target_pairs={{0,17},{1,16},{2,19},{3,18},{4,21},{5,20},{6,23},{7,22},{8,25},{9,... | collective-permute-start | bytes 196616 | tf_op jit(solution)/shard_map/ppermute | solution.py:736
  233.7 12.3 %collective-permute-start.29 = (bf16[64,512]{1,0:T(8,128)(2,1)}, bf16[64,512]{1,0:T(8,128)(2,1)}, u32[]{:S(2)}, u32[]{:S(2)}) collective-permute-start(bf16[64,512]{1,0:T(8,128)(2,1)} %get-tuple-element.80), channel_id=1, source_target_pairs={{0,1},{1,0},{2,3},{3,2},{4,5},{5,4},{6,7},{7,6},{8,9},{9,8},{10,11... | collective-permute-start | bytes 196616 | tf_op jit(solution)/shard_map/ppermute | solution.py:736
  234.4 11.6 %collective-permute-start.28 = (bf16[64,512]{1,0:T(8,128)(2,1)}, bf16[64,512]{1,0:T(8,128)(2,1)}, u32[]{:S(2)}, u32[]{:S(2)}) collective-permute-start(bf16[64,512]{1,0:T(8,128)(2,1)} %get-tuple-element.81), channel_id=1, source_target_pairs={{0,16},{1,17},{2,18},{3,19},{4,20},{5,21},{6,22},{7,23},{8,24},{9,... | collective-permute-start | bytes 196616 | tf_op jit(solution)/shard_map/ppermute | solution.py:736
  235.0 11.0 %collective-permute-start.33 = (bf16[144,512]{1,0:T(8,128)(2,1)S(1)}, bf16[144,512]{1,0:T(8,128)(2,1)S(1)}, u32[]{:S(2)}, u32[]{:S(2)}) collective-permute-start(bf16[144,512]{1,0:T(8,128)(2,1)S(1)} %get-tuple-element.76), channel_id=1, source_target_pairs={{0,6},{1,7},{2,4},{3,5},{4,2},{5,3},{6,0},{7,1},{8,14},{9,15},{10,... | collective-permute-start | bytes 442376 | tf_op jit(solution)/shard_map/ppermute | solution.py:736
  237.7 11.5 %collective-permute-start.32 = (bf16[144,512]{1,0:T(8,128)(2,1)S(1)}, bf16[144,512]{1,0:T(8,128)(2,1)}, u32[]{:S(2)}, u32[]{:S(2)}) collective-permute-start(bf16[144,512]{1,0:T(8,128)(2,1)S(1)} %get-tuple-element.77), channel_id=1, source_target_pairs={{0,4},{1,5},{2,6},{3,7},{4,0},{5,1},{6,2},{7,3},{8,12},{9,13},{10,... | collective-permute-start | bytes 442376 | tf_op jit(solution)/shard_map/ppermute | solution.py:736
  237.7 11.5 %collective-permute-start.31 = (bf16[144,512]{1,0:T(8,128)(2,1)S(1)}, bf16[144,512]{1,0:T(8,128)(2,1)}, u32[]{:S(2)}, u32[]{:S(2)}) collective-permute-start(bf16[144,512]{1,0:T(8,128)(2,1)S(1)} %get-tuple-element.78), channel_id=1, source_target_pairs={{0,2},{1,3},{2,0},{3,1},{4,6},{5,7},{6,4},{7,5},{8,10},{9,11},{10,... | collective-permute-start | bytes 442376 | tf_op jit(solution)/shard_map/ppermute | solution.py:736
  246.0 24.8 %copy-start.3 = (f32[98464]{0:T(1024)S(1)}, f32[98464]{0:T(1024)}, u32[]{:S(2)}) copy-start(f32[98464]{0:T(1024)} %param.11) | copy-start | bytes 1181572
  246.0 24.8 %copy-start.13 = (f32[98464]{0:T(1024)S(1)}, f32[98464]{0:T(1024)}, u32[]{:S(2)}) copy-start(f32[98464]{0:T(1024)} %param.12) | copy-start | bytes 1181572
  246.0 24.8 %copy-start.14 = (f32[98464]{0:T(1024)S(1)}, f32[98464]{0:T(1024)}, u32[]{:S(2)}) copy-start(f32[98464]{0:T(1024)} %param.13) | copy-start | bytes 1181572
  253.2 1.2 collective-permute-start.34
  255.1 4.6 %collective-permute-start.37 = (f32[8,128]{1,0:T(8,128)S(1)}, f32[8,128]{1,0:T(8,128)S(1)}, u32[]{:S(2)}, u32[]{:S(2)}) collective-permute-start(f32[8,128]{1,0:T(8,128)S(1)} %broadcast_add_fusion), channel_id=1, source_target_pairs={{0,17},{1,16},{2,19},{3,18},{4,21},{5,20},{6,23},{7,22},{8,25},{9,... | collective-permute-start | bytes 12296 | tf_op jit(solution)/shard_map/ppermute | solution.py:736
  257.3 3.6 %collective-permute-start.36 = (f32[8,128]{1,0:T(8,128)S(1)}, f32[8,128]{1,0:T(8,128)S(1)}, u32[]{:S(2)}, u32[]{:S(2)}) collective-permute-start(f32[8,128]{1,0:T(8,128)S(1)} %broadcast_add_fusion), channel_id=1, source_target_pairs={{0,1},{1,0},{2,3},{3,2},{4,5},{5,4},{6,7},{7,6},{8,9},{9,8},{10,11... | collective-permute-start | bytes 12296 | tf_op jit(solution)/shard_map/ppermute | solution.py:736
  258.2 3.6 %collective-permute-start.35 = (f32[8,128]{1,0:T(8,128)S(1)}, f32[8,128]{1,0:T(8,128)S(1)}, u32[]{:S(2)}, u32[]{:S(2)}) collective-permute-start(f32[8,128]{1,0:T(8,128)S(1)} %broadcast_add_fusion), channel_id=1, source_target_pairs={{0,16},{1,17},{2,18},{3,19},{4,20},{5,21},{6,22},{7,23},{8,24},{9,... | collective-permute-start | bytes 12296 | tf_op jit(solution)/shard_map/ppermute | solution.py:736
  262.4 5.5 %collective-permute-start.40 = (f32[8,128]{1,0:T(8,128)S(1)}, f32[8,128]{1,0:T(8,128)S(1)}, u32[]{:S(2)}, u32[]{:S(2)}) collective-permute-start(f32[8,128]{1,0:T(8,128)S(1)} %add_add_fusion.1), channel_id=1, source_target_pairs={{0,6},{1,7},{2,4},{3,5},{4,2},{5,3},{6,0},{7,1},{8,14},{9,15},{10,... | collective-permute-start | bytes 12296 | tf_op jit(solution)/shard_map/ppermute | solution.py:736
  265.0 4.5 %collective-permute-start.39 = (f32[8,128]{1,0:T(8,128)S(1)}, f32[8,128]{1,0:T(8,128)S(1)}, u32[]{:S(2)}, u32[]{:S(2)}) collective-permute-start(f32[8,128]{1,0:T(8,128)S(1)} %add_add_fusion.1), channel_id=1, source_target_pairs={{0,4},{1,5},{2,6},{3,7},{4,0},{5,1},{6,2},{7,3},{8,12},{9,13},{10,... | collective-permute-start | bytes 12296 | tf_op jit(solution)/shard_map/ppermute | solution.py:736
  265.0 4.5 %collective-permute-start.38 = (f32[8,128]{1,0:T(8,128)S(1)}, f32[8,128]{1,0:T(8,128)S(1)}, u32[]{:S(2)}, u32[]{:S(2)}) collective-permute-start(f32[8,128]{1,0:T(8,128)S(1)} %add_add_fusion.1), channel_id=1, source_target_pairs={{0,2},{1,3},{2,0},{3,1},{4,6},{5,7},{6,4},{7,5},{8,10},{9,11},{10,... | collective-permute-start | bytes 12296 | tf_op jit(solution)/shard_map/ppermute | solution.py:736
  (16 other events, 79.6 us)
where the time goes:
time: 279 us; the launch traced here: 275 us
  Pallas kernels  127 us (46%)
  starting transfers between devices  65.7 us (24%)
  waiting for transfers between devices  55.5 us (20%)
  other arithmetic  15 us (5%)
  local copies, waits for them, and re-layouts  6.73 us (2%)
  between operations  4.06 us (1%)
    pallas_call x1, Pallas kernels, layer(): pl.pallas_call(layer_kernel, out_shape=(shape_of(SEQ, D), shape_of(SEQ, D...  108 us
    ppermute x41, starting transfers between devices, send(): return lax.ppermute(array, ('dp', 'fsdp'), pairs)  65.7 us
    ppermute x41, waiting for transfers between devices, send(): return lax.ppermute(array, ('dp', 'fsdp'), pairs)  55.5 us
    pallas_call x2, Pallas kernels, restore(): pl.pallas_call(restore_kernel, out_shape=jax.ShapeDtypeStruct((SEQ, D), f...  13.1 us
    pallas_call x1, Pallas kernels, prepare(): pl.pallas_call(prepare_kernel, out_shape=(jax.ShapeDtypeStruct((8, SEQ),...  5.8 us
  transfers between devices with their start and end apart: 41, of which 15 were waited for; matrix products, arithmetic and copies ran while one was open for 2% of the time, Pallas kernels for 7%

commit v1 on v0

--- a/solution.py
+++ b/solution.py
@@ -36,7 +36,7 @@
 SIZES_LENGTH = (512,)
 SIZES_ATTEND = (256, 128)
 SIZES_SHIFTED = (128,)
-SIZES_ATTEND_BACK = (256, 128)
+SIZES_ATTEND_BACK = (256,)
 SIZES_FEED = (512, 128)
 SIZES_BACK = (512, 128)
 PAIRS = HEADS // 2
@@ -306,12 +306,29 @@
                     copy.start()
                     arriving.append(copy)
 
-    for total in (qkv_sum, out_sum, up_sum, down_sum, vector_sum):
-        total[...] = jnp.zeros_like(total)
-
-    mixed[...] = jnp.zeros_like(mixed)
-    state[0] = states_ref[...].astype(f32)
-    state[1] = jnp.zeros((SEQ, D), f32)
+    def start_rows(n, carried):
+        rows = at_rows(n * UNIT, UNIT)
+        state[0, rows, :] = states_ref[rows, :].astype(f32)
+        state[1, rows, :] = jnp.zeros((UNIT, D), f32)
+        mixed[0, rows, :] = jnp.zeros((UNIT, D), bf16)
+        mixed[1, rows, :] = jnp.zeros((UNIT, D), bf16)
+        mixed_grad[rows, :] = jnp.zeros((UNIT, D), bf16)
+        return carried
+
+    lax.fori_loop(0, SEQ // UNIT, start_rows, 0)
+
+    def start_sums(n, carried):
+        rows = at_rows(n * UNIT, UNIT)
+        for total in (qkv_sum, up_sum, down_sum):
+            for j in range(total.shape[0]):
+                total[j, rows, :] = jnp.zeros((UNIT, D), f32)
+        out_sum[rows, :] = jnp.zeros((UNIT, D), f32)
+        return carried
+
+    lax.fori_loop(0, D // UNIT, start_sums, 0)
+    vector_sum[...] = jnp.zeros_like(vector_sum)
+    centres[...] = jnp.zeros_like(centres)
+    logs[...] = jnp.full_like(logs, 1e30)
     for copy in arriving:
         copy.wait()
 
@@ -366,9 +383,13 @@
     def attend_pair(step, start, size, pair, shifted):
         rows = at_rows(start, size)
         ones = jnp.where(iota((SEQ, 1), 0) < length, 1.0, 0.0).astype(bf16)
-        queries = projected[step, rows, pl.ds(pair * PAIR, PAIR)]
-        keys = projected[step, :, pl.ds(D + pair * PAIR, PAIR)]
-        values = projected[step, :, pl.ds(2 * D + pair * PAIR, PAIR)]
+        def lanes(offset):
+            at = offset + pair * PAIR
+            return pl.ds(at if isinstance(at, int) else pl.multiple_of(at, PAIR), PAIR)
+
+        queries = projected[step, rows, lanes(0)]
+        keys = projected[step, :, lanes(D)]
+        values = projected[step, :, lanes(2 * D)]
         peaks, sums = [], []
         for half in range(2):
             scores = dot_nt(jnp.where(own[half], queries, jnp.zeros_like(queries)), keys) * SCORE_LOG2
@@ -377,7 +398,7 @@
                 scores = scores - peaks[half]
             sums.append(dot(jnp.exp2(scores).astype(bf16), jnp.where(own[half], values, ones)))
         total = jnp.where(lower, pltpu.roll(sums[0], 64, 1), pltpu.roll(sums[1], 64, 1))
-        mixed[step, rows, pl.ds(pair * PAIR, PAIR)] = (jnp.where(lower, sums[0], sums[1]) / total).astype(bf16)
+        mixed[step, rows, lanes(0)] = (jnp.where(lower, sums[0], sums[1]) / total).astype(bf16)
         log = jnp.log2(total)
         if shifted:
             log = log + jnp.where(lower, peaks[0], peaks[1])
@@ -394,8 +415,15 @@
         @pl.when(plain)
         def _():
             def body(start, size):
-                for pair in range(PAIRS):
+                def each(pair, carried):
                     attend_pair(step, start, size, pair, False)
+                    return carried
+
+                if size == SIZES_ATTEND[0]:
+                    for pair in range(PAIRS):
+                        each(pair, 0)
+                else:
+                    lax.fori_loop(0, PAIRS, each, 0)
 
             over_rows(query_rows(step), SIZES_ATTEND, body)
 
@@ -403,7 +431,7 @@
         def _():
             def body(start, size):
                 def each(pair, carried):
-                    attend_pair(step, start, size, pl.multiple_of(pair, 1), True)
+                    attend_pair(step, start, size, pair, True)
                     return carried
 
                 lax.fori_loop(0, PAIRS, each, 0)
@@ -605,7 +633,16 @@
     for j in range(4):
         for at, rows, first in UP_SEGMENTS:
             place(2048 + at + rows * j, rows, up_sum[j, first : first + rows, :].astype(bf16))
-        place(4096 + D * j, D, down_sum[j].T.astype(bf16))
+
+    def place_down(j, carried):
+        value = down_sum[j].T.astype(bf16)
+        for part in range(D // 64):
+            row = 4096 + D * j + 64 * part
+            at = pl.multiple_of(row // CHUNK * PACKED + row % CHUNK, 16)
+            hidden[pl.ds(at, 64), :] = value[64 * part : 64 * (part + 1)]
+        return carried
+
+    lax.fori_loop(0, 4, place_down, 0)
     for n in range(DEVICES):
         extra = next_rows(n, qkv_sum, out_sum, up_sum, hidden, vector_sum).astype(bf16)
         hidden[PACKED * n + CHUNK : PACKED * (n + 1), :] = extra

time: 279 us -> 289 us (1.036)
  Pallas kernels: 127 us -> 140 us
    pallas_call x1, Pallas kernels: 108 us -> 121 us  [layer(): pl.pallas_call(layer_kernel, out_shape=(shape_of(SEQ, D), shape_of(SEQ, D...]
  transfers between devices with their start and end apart: 41 -> 41, of which waited for: 15 -> 14; matrix products, arithmetic and copies ran while one was open for 2% -> 2% of each run, Pallas kernels for 7% -> 7%
where the time goes in v1:
time: 289 us; the launch traced here: 288 us
  Pallas kernels  140 us (48%)
  starting transfers between devices  67.6 us (23%)
  waiting for transfers between devices  54 us (19%)
  other arithmetic  15 us (5%)
  local copies, waits for them, and re-layouts  6.7 us (2%)
  between operations  3.62 us (1%)
    pallas_call x1, Pallas kernels, layer(): pl.pallas_call(layer_kernel, out_shape=(shape_of(SEQ, D), shape_of(SEQ, D...  121 us
    ppermute x41, starting transfers between devices, send(): return lax.ppermute(array, ('dp', 'fsdp'), pairs)  67.6 us
    ppermute x41, waiting for transfers between devices, send(): return lax.ppermute(array, ('dp', 'fsdp'), pairs)  54 us
    pallas_call x2, Pallas kernels, restore(): pl.pallas_call(restore_kernel, out_shape=jax.ShapeDtypeStruct((SEQ, D), f...  13.1 us
    pallas_call x1, Pallas kernels, prepare(): pl.pallas_call(prepare_kernel, out_shape=(jax.ShapeDtypeStruct((8, SEQ),...  5.8 us
  transfers between devices with their start and end apart: 41, of which 14 were waited for; matrix products, arithmetic and copies ran while one was open for 2% of the time, Pallas kernels for 7%

profile of v1, /device:TPU:0, one launch (start us, length us, event | category | flops | bytes accessed | tf_op | source)
XLA Modules:
  0.0 287.6 jit_solution(2293579971570278418)
XLA Ops:
  0.7 1.0 convert_element_type.77
  1.7 1.3 concatenate.6
  4.3 3.0 %collective-permute-start.1 = (bf16[64,512]{1,0:T(8,128)(2,1)S(1)}, bf16[64,512]{1,0:T(8,128)(2,1)S(1)}, u32[]{:S(2)}, u32[]{:S(2)}) collective-permute-start(bf16[64,512]{1,0:T(8,128)(2,1)S(1)} %get-tuple-element.85), channel_id=1, source_target_pairs={{0,1},{1,0},{2,3},{3,2},{4,5},{5,4},{6,7},{7,6},{8,9},{9,8},{10,11... | collective-permute-start | bytes 196616 | tf_op jit(solution)/shard_map/ppermute | solution.py:773
  7.3 1.5 collective-permute-start
  8.9 3.1 %collective-permute-start.4 = (bf16[144,512]{1,0:T(8,128)(2,1)S(1)}, bf16[144,512]{1,0:T(8,128)(2,1)S(1)}, u32[]{:S(2)}, u32[]{:S(2)}) collective-permute-start(bf16[144,512]{1,0:T(8,128)(2,1)S(1)} %get-tuple-element.83), channel_id=1, source_target_pairs={{0,4},{1,5},{2,6},{3,7},{4,0},{5,1},{6,2},{7,3},{8,12},{9,13},{10,... | collective-permute-start | bytes 442376 | tf_op jit(solution)/shard_map/ppermute | solution.py:773
  12.0 1.6 collective-permute-start.3
  14.9 5.8 %prepare.1 = (f32[8,1024]{1,0:T(8,128)}, bf16[1024,512]{1,0:T(8,128)(2,1)}, bf16[1024,512]{1,0:T(8,128)(2,1)}, s32[6]{0:T(128)}) custom-call(s32[1]{0:T(128)S(6)} %copy.20.length_ref, s32[4]{0:T(128)} %pad_add_fusion.index_ref, s32[1,1024]{1,0:T(1,128)} %count_ref.1, bf16[1024,512]{1,0:T(8,128)(2,1)} %bitcast.60, bf16[1024,512]{1,0:T(8,128)(2,1)} %bitcast.61), custom_call_target="tpu_custom_call" | custom-call | flops 6000000000 | bytes 4000000 | tf_op jit(solution)/shard_map/prepare/pallas_call | solution.py:140
  20.7 1.8 collective-permute-done.4
  22.7 2.5 collective-permute-start.15
  26.3 2.9 collective-permute-start.8
  29.2 1.8 collective-permute-start.7
  30.9 6.5 %collective-permute-done.8.refs_3_ = bf16[4,64,512]{2,1,0:T(8,128)(2,1)S(1)} collective-permute-done((bf16[4,64,512]{2,1,0:T(8,128)(2,1)S(1)}, bf16[4,64,512]{2,1,0:T(8,128)(2,1)S(1)}, u32[]{:S(2)}, u32[]{:S(2)}) %collective-permute-start.8) | collective-permute-done | bytes 262176 | tf_op jit(solution)/shard_map/ppermute | solution.py:773
  37.4 10.4 %collective-permute-start.6 = (bf16[4,64,512]{2,1,0:T(8,128)(2,1)S(1)}, bf16[4,64,512]{2,1,0:T(8,128)(2,1)S(1)}, u32[]{:S(2)}, u32[]{:S(2)}) collective-permute-start(bf16[4,64,512]{2,1,0:T(8,128)(2,1)S(1)} %pad_maximum_fusion.1.refs_0_), channel_id=1, source_target_pairs={{0,2},{1,3},{2,0},{3,1},{4,6},{5,7},{6,4},{7,5},{8,10},{9,11},{10,... | collective-permute-start | bytes 786440 | tf_op jit(solution)/shard_map/ppermute | solution.py:773
  47.8 5.1 %collective-permute-done.7.refs_2_ = bf16[4,64,512]{2,1,0:T(8,128)(2,1)S(1)} collective-permute-done((bf16[4,64,512]{2,1,0:T(8,128)(2,1)S(1)}, bf16[4,64,512]{2,1,0:T(8,128)(2,1)S(1)}, u32[]{:S(2)}, u32[]{:S(2)}) %collective-permute-start.7) | collective-permute-done | bytes 262176 | tf_op jit(solution)/shard_map/ppermute | solution.py:773
  52.9 5.5 %collective-permute-done.6.refs_1_ = bf16[4,64,512]{2,1,0:T(8,128)(2,1)S(1)} collective-permute-done((bf16[4,64,512]{2,1,0:T(8,128)(2,1)S(1)}, bf16[4,64,512]{2,1,0:T(8,128)(2,1)S(1)}, u32[]{:S(2)}, u32[]{:S(2)}) %collective-permute-start.6) | collective-permute-done | bytes 262176 | tf_op jit(solution)/shard_map/ppermute | solution.py:773
  59.5 3.8 %collective-permute-done.11.refs_6_ = bf16[4,64,512]{2,1,0:T(8,128)(2,1)S(1)} collective-permute-done((bf16[4,64,512]{2,1,0:T(8,128)(2,1)S(1)}, bf16[4,64,512]{2,1,0:T(8,128)(2,1)S(1)}, u32[]{:S(2)}, u32[]{:S(2)}) %collective-permute-start.11) | collective-permute-done | bytes 262176 | tf_op jit(solution)/shard_map/ppermute | solution.py:773
  63.4 1.4 collective-permute-done.10.refs_5_
  66.8 121.1 %layer.1 = (f32[1024,512]{1,0:T(8,128)}, f32[1024,512]{1,0:T(8,128)}, bf16[16,64,512]{2,1,0:T(8,128)(2,1)}, bf16[16,64,512]{2,1,0:T(8,128)(2,1)}, bf16[16,144,51...) custom-call(s32[6]{0:T(128)} %get-tuple-element.41.meta, ...), custom_call_target="tpu_custom_call" | custom-call | tf_op jit(solution)/shard_map/layer/pallas_call | solution.py:671
  188.4 6.6 %restore_final.1 = f32[1024,512]{1,0:T(8,128)} custom-call(f32[8,1024]{1,0:T(8,128)} %get-tuple-element.47.place_ref, f32[1024,512]{1,0:T(8,128)} %get-tuple-element.48.sorted_ref), custom_call_target="tpu_custom_call" | custom-call | flops 6000000000 | bytes 4000000 | tf_op jit(solution)/shard_map/restore_final/pallas_call | solution.py:187
  195.0 2.1 slice_add_fusion.6
  197.2 1.5 slice_add_fusion.2
  199.6 16.0 %collective-permute-start.27 = (bf16[4,144,512]{2,1,0:T(8,128)(2,1)}, bf16[4,144,512]{2,1,0:T(8,128)(2,1)}, u32[]{:S(2)}, u32[]{:S(2)}) collective-permute-start(bf16[4,144,512]{2,1,0:T(8,128)(2,1)} %get-tuple-element.71), channel_id=1, source_target_pairs={{0,17},{1,16},{2,19},{3,18},{4,21},{5,20},{6,23},{7,22},{8,25},{9,... | collective-permute-start | bytes 1769480 | tf_op jit(solution)/shard_map/ppermute | solution.py:773
  215.6 3.4 %collective-permute-start.23 = (bf16[4,64,512]{2,1,0:T(8,128)(2,1)}, bf16[4,64,512]{2,1,0:T(8,128)(2,1)S(1)}, u32[]{:S(2)}, u32[]{:S(2)}) collective-permute-start(bf16[4,64,512]{2,1,0:T(8,128)(2,1)} %get-tuple-element.74), channel_id=1, source_target_pairs={{0,6},{1,7},{2,4},{3,5},{4,2},{5,3},{6,0},{7,1},{8,14},{9,15},{10,... | collective-permute-start | bytes 786440 | tf_op jit(solution)/shard_map/ppermute | solution.py:773
  219.0 2.0 collective-permute-start.22
  221.0 5.9 %collective-permute-done.23 = bf16[4,64,512]{2,1,0:T(8,128)(2,1)S(1)} collective-permute-done((bf16[4,64,512]{2,1,0:T(8,128)(2,1)}, bf16[4,64,512]{2,1,0:T(8,128)(2,1)S(1)}, u32[]{:S(2)}, u32[]{:S(2)}) %collective-permute-start.23) | collective-permute-done | bytes 262176 | tf_op jit(solution)/shard_map/ppermute | solution.py:773
  226.9 15.1 %collective-permute-done.22 = bf16[4,64,512]{2,1,0:T(8,128)(2,1)S(1)} collective-permute-done((bf16[4,64,512]{2,1,0:T(8,128)(2,1)}, bf16[4,64,512]{2,1,0:T(8,128)(2,1)S(1)}, u32[]{:S(2)}, u32[]{:S(2)}) %collective-permute-start.22) | collective-permute-done | bytes 262176 | tf_op jit(solution)/shard_map/ppermute | solution.py:773
  242.0 1.2 convert_add_fusion.1
  243.3 2.0 convert_add_fusion
  245.9 1.0 collective-permute-start.30
  247.7 1.7 collective-permute-start.28
  249.5 2.7 collective-permute-start.33
  252.3 1.7 collective-permute-start.31
  254.0 6.5 %restore_grad.1 = f32[1024,512]{1,0:T(8,128)} custom-call(f32[8,1024]{1,0:T(8,128)} %get-tuple-element.47.place_ref, f32[1024,512]{1,0:T(8,128)} %get-tuple-element.57.sorted_ref), custom_call_target="tpu_custom_call" | custom-call | flops 6000000000 | bytes 4000000 | tf_op jit(solution)/shard_map/restore_grad/pallas_call | solution.py:187
  260.5 3.2 %collective-permute-done.32 = bf16[144,512]{1,0:T(8,128)(2,1)} collective-permute-done((bf16[144,512]{1,0:T(8,128)(2,1)S(1)}, bf16[144,512]{1,0:T(8,128)(2,1)}, u32[]{:S(2)}, u32[]{:S(2)}) %collective-permute-start.32) | collective-permute-done | bytes 147488 | tf_op jit(solution)/shard_map/ppermute | solution.py:773
  263.8 1.0 fusion.5
  264.8 0.9 fusion.7
  267.8 1.2 collective-permute-done.34
  269.6 0.9 collective-permute-start.37
  270.5 0.9 collective-permute-start.36
  271.5 1.7 collective-permute-start.35
  273.1 1.0 collective-permute-done.37
  274.2 0.9 collective-permute-done.35
  275.7 2.5 collective-permute-start.40
  278.3 1.9 collective-permute-start.38
  280.2 1.0 collective-permute-done.40
  281.2 1.6 collective-permute-done.39
  284.1 1.5 fusion.11
  285.6 0.9 multiply_add_fusion
  (116 shorter events, 13.2 us)
Async XLA Ops:
  4.3 10.5 %collective-permute-start.1 = (bf16[64,512]{1,0:T(8,128)(2,1)S(1)}, bf16[64,512]{1,0:T(8,128)(2,1)S(1)}, u32[]{:S(2)}, u32[]{:S(2)}) collective-permute-start(bf16[64,512]{1,0:T(8,128)(2,1)S(1)} %get-tuple-element.85), channel_id=1, source_target_pairs={{0,1},{1,0},{2,3},{3,2},{4,5},{5,4},{6,7},{7,6},{8,9},{9,8},{10,11... | collective-permute-start | bytes 196616 | tf_op jit(solution)/shard_map/ppermute | solution.py:773
  7.3 13.3 %collective-permute-start = (bf16[64,512]{1,0:T(8,128)(2,1)S(1)}, bf16[64,512]{1,0:T(8,128)(2,1)S(1)}, u32[]{:S(2)}, u32[]{:S(2)}) collective-permute-start(bf16[64,512]{1,0:T(8,128)(2,1)S(1)} %get-tuple-element.85), channel_id=1, source_target_pairs={{0,16},{1,17},{2,18},{3,19},{4,20},{5,21},{6,22},{7,23},{8,24},{9,... | collective-permute-start | bytes 196616 | tf_op jit(solution)/shard_map/ppermute | solution.py:773
  8.9 11.8 %collective-permute-start.2 = (bf16[64,512]{1,0:T(8,128)(2,1)S(1)}, bf16[64,512]{1,0:T(8,128)(2,1)S(1)}, u32[]{:S(2)}, u32[]{:S(2)}) collective-permute-start(bf16[64,512]{1,0:T(8,128)(2,1)S(1)} %get-tuple-element.85), channel_id=1, source_target_pairs={{0,17},{1,16},{2,19},{3,18},{4,21},{5,20},{6,23},{7,22},{8,25},{9,... | collective-permute-start | bytes 196616 | tf_op jit(solution)/shard_map/ppermute | solution.py:773
  8.9 13.7 %collective-permute-start.4 = (bf16[144,512]{1,0:T(8,128)(2,1)S(1)}, bf16[144,512]{1,0:T(8,128)(2,1)S(1)}, u32[]{:S(2)}, u32[]{:S(2)}) collective-permute-start(bf16[144,512]{1,0:T(8,128)(2,1)S(1)} %get-tuple-element.83), channel_id=1, source_target_pairs={{0,4},{1,5},{2,6},{3,7},{4,0},{5,1},{6,2},{7,3},{8,12},{9,13},{10,... | collective-permute-start | bytes 442376 | tf_op jit(solution)/shard_map/ppermute | solution.py:773
  12.0 10.6 %collective-permute-start.3 = (bf16[144,512]{1,0:T(8,128)(2,1)S(1)}, bf16[144,512]{1,0:T(8,128)(2,1)S(1)}, u32[]{:S(2)}, u32[]{:S(2)}) collective-permute-start(bf16[144,512]{1,0:T(8,128)(2,1)S(1)} %get-tuple-element.83), channel_id=1, source_target_pairs={{0,2},{1,3},{2,0},{3,1},{4,6},{5,7},{6,4},{7,5},{8,10},{9,11},{10,... | collective-permute-start | bytes 442376 | tf_op jit(solution)/shard_map/ppermute | solution.py:773
  14.9 7.7 %collective-permute-start.5 = (bf16[144,512]{1,0:T(8,128)(2,1)S(1)}, bf16[144,512]{1,0:T(8,128)(2,1)S(1)}, u32[]{:S(2)}, u32[]{:S(2)}) collective-permute-start(bf16[144,512]{1,0:T(8,128)(2,1)S(1)} %get-tuple-element.83), channel_id=1, source_target_pairs={{0,6},{1,7},{2,4},{3,5},{4,2},{5,3},{6,0},{7,1},{8,14},{9,15},{10,... | collective-permute-start | bytes 442376 | tf_op jit(solution)/shard_map/ppermute | solution.py:773
  20.7 46.0 %copy-start.5 = (bf16[4,64,512]{2,1,0:T(8,128)(2,1)}, bf16[4,64,512]{2,1,0:T(8,128)(2,1)S(1)}, u32[]{:S(2)}) copy-start(bf16[4,64,512]{2,1,0:T(8,128)(2,1)S(1)} %pad_maximum_fusion.1.refs_0_) | copy-start | bytes 786436
  22.7 44.1 %copy-start = (bf16[4,144,512]{2,1,0:T(8,128)(2,1)}, bf16[4,144,512]{2,1,0:T(8,128)(2,1)S(1)}, u32[]{:S(2)}) copy-start(bf16[4,144,512]{2,1,0:T(8,128)(2,1)S(1)} %pad_maximum_fusion.refs_8_) | copy-start | bytes 1769476
  22.7 6.5 %collective-permute-start.9 = (bf16[4,64,512]{2,1,0:T(8,128)(2,1)S(1)}, bf16[4,64,512]{2,1,0:T(8,128)(2,1)S(1)}, u32[]{:S(2)}, u32[]{:S(2)}) collective-permute-start(bf16[4,64,512]{2,1,0:T(8,128)(2,1)S(1)} %pad_maximum_fusion.1.refs_0_), channel_id=1, source_target_pairs={{0,8},{1,9},{2,10},{3,11},{4,12},{5,13},{6,14},{7,15},{8,0},{9,1},... | collective-permute-start | bytes 786440 | tf_op jit(solution)/shard_map/ppermute | solution.py:773
  22.7 35.7 %collective-permute-start.15 = (bf16[4,144,512]{2,1,0:T(8,128)(2,1)S(1)}, bf16[4,144,512]{2,1,0:T(8,128)(2,1)S(1)}, u32[]{:S(2)}, u32[]{:S(2)}) collective-permute-start(bf16[4,144,512]{2,1,0:T(8,128)(2,1)S(1)} %pad_maximum_fusion.refs_8_), channel_id=1, source_target_pairs={{0,17},{1,16},{2,19},{3,18},{4,21},{5,20},{6,23},{7,22},{8,25},{9,... | collective-permute-start | bytes 1769480 | tf_op jit(solution)/shard_map/ppermute | solution.py:773
  25.3 33.6 %collective-permute-start.14 = (bf16[4,144,512]{2,1,0:T(8,128)(2,1)S(1)}, bf16[4,144,512]{2,1,0:T(8,128)(2,1)S(1)}, u32[]{:S(2)}, u32[]{:S(2)}) collective-permute-start(bf16[4,144,512]{2,1,0:T(8,128)(2,1)S(1)} %pad_maximum_fusion.refs_8_), channel_id=1, source_target_pairs={{0,1},{1,0},{2,3},{3,2},{4,5},{5,4},{6,7},{7,6},{8,9},{9,8},{10,11... | collective-permute-start | bytes 1769480 | tf_op jit(solution)/shard_map/ppermute | solution.py:773
  25.8 33.2 %collective-permute-start.13 = (bf16[4,144,512]{2,1,0:T(8,128)(2,1)S(1)}, bf16[4,144,512]{2,1,0:T(8,128)(2,1)S(1)}, u32[]{:S(2)}, u32[]{:S(2)}) collective-permute-start(bf16[4,144,512]{2,1,0:T(8,128)(2,1)S(1)} %pad_maximum_fusion.refs_8_), channel_id=1, source_target_pairs={{0,16},{1,17},{2,18},{3,19},{4,20},{5,21},{6,22},{7,23},{8,24},{9,... | collective-permute-start | bytes 1769480 | tf_op jit(solution)/shard_map/ppermute | solution.py:773
  26.3 11.1 %collective-permute-start.8 = (bf16[4,64,512]{2,1,0:T(8,128)(2,1)S(1)}, bf16[4,64,512]{2,1,0:T(8,128)(2,1)S(1)}, u32[]{:S(2)}, u32[]{:S(2)}) collective-permute-start(bf16[4,64,512]{2,1,0:T(8,128)(2,1)S(1)} %pad_maximum_fusion.1.refs_0_), channel_id=1, source_target_pairs={{0,6},{1,7},{2,4},{3,5},{4,2},{5,3},{6,0},{7,1},{8,14},{9,15},{10,... | collective-permute-start | bytes 786440 | tf_op jit(solution)/shard_map/ppermute | solution.py:773
  29.2 23.7 %copy-start.16 = (bf16[4,64,512]{2,1,0:T(8,128)(2,1)}, bf16[4,64,512]{2,1,0:T(8,128)(2,1)S(1)}, u32[]{:S(2)}) copy-start(bf16[4,64,512]{2,1,0:T(8,128)(2,1)S(1)} %collective-permute-done.9.refs_4_) | copy-start | bytes 786436
  29.2 23.7 %collective-permute-start.7 = (bf16[4,64,512]{2,1,0:T(8,128)(2,1)S(1)}, bf16[4,64,512]{2,1,0:T(8,128)(2,1)S(1)}, u32[]{:S(2)}, u32[]{:S(2)}) collective-permute-start(bf16[4,64,512]{2,1,0:T(8,128)(2,1)S(1)} %pad_maximum_fusion.1.refs_0_), channel_id=1, source_target_pairs={{0,4},{1,5},{2,6},{3,7},{4,0},{5,1},{6,2},{7,3},{8,12},{9,13},{10,... | collective-permute-start | bytes 786440 | tf_op jit(solution)/shard_map/ppermute | solution.py:773
  37.4 27.5 %copy-start.17 = (bf16[4,64,512]{2,1,0:T(8,128)(2,1)}, bf16[4,64,512]{2,1,0:T(8,128)(2,1)S(1)}, u32[]{:S(2)}) copy-start(bf16[4,64,512]{2,1,0:T(8,128)(2,1)S(1)} %collective-permute-done.8.refs_3_) | copy-start | bytes 786436
  37.4 21.0 %collective-permute-start.6 = (bf16[4,64,512]{2,1,0:T(8,128)(2,1)S(1)}, bf16[4,64,512]{2,1,0:T(8,128)(2,1)S(1)}, u32[]{:S(2)}, u32[]{:S(2)}) collective-permute-start(bf16[4,64,512]{2,1,0:T(8,128)(2,1)S(1)} %pad_maximum_fusion.1.refs_0_), channel_id=1, source_target_pairs={{0,2},{1,3},{2,0},{3,1},{4,6},{5,7},{6,4},{7,5},{8,10},{9,11},{10,... | collective-permute-start | bytes 786440 | tf_op jit(solution)/shard_map/ppermute | solution.py:773
  52.9 6.6 %collective-permute-start.12 = (bf16[4,64,512]{2,1,0:T(8,128)(2,1)S(1)}, bf16[4,64,512]{2,1,0:T(8,128)(2,1)S(1)}, u32[]{:S(2)}, u32[]{:S(2)}) collective-permute-start(bf16[4,64,512]{2,1,0:T(8,128)(2,1)S(1)} %collective-permute-done.8.refs_3_), channel_id=1, source_target_pairs={{0,8},{1,9},{2,10},{3,11},{4,12},{5,13},{6,14},{7,15},{8,0},{9,1},... | collective-permute-start | bytes 786440 | tf_op jit(solution)/shard_map/ppermute | solution.py:773
  58.4 6.5 %collective-permute-start.16 = (bf16[4,144,512]{2,1,0:T(8,128)(2,1)S(1)}, bf16[4,144,512]{2,1,0:T(8,128)(2,1)S(1)}, u32[]{:S(2)}, u32[]{:S(2)}) collective-permute-start(bf16[4,144,512]{2,1,0:T(8,128)(2,1)S(1)} %pad_maximum_fusion.refs_8_), channel_id=1, source_target_pairs={{0,8},{1,9},{2,10},{3,11},{4,12},{5,13},{6,14},{7,15},{8,0},{9,1},... | collective-permute-start | bytes 1769480 | tf_op jit(solution)/shard_map/ppermute | solution.py:773
  58.4 6.4 %collective-permute-start.19 = (bf16[4,144,512]{2,1,0:T(8,128)(2,1)S(1)}, bf16[4,144,512]{2,1,0:T(8,128)(2,1)S(1)}, u32[]{:S(2)}, u32[]{:S(2)}) collective-permute-start(bf16[4,144,512]{2,1,0:T(8,128)(2,1)S(1)} %collective-permute-done.15.refs_11_), channel_id=1, source_target_pairs={{0,8},{1,9},{2,10},{3,11},{4,12},{5,13},{6,14},{7,15},{8,0},{9,1},... | collective-permute-start | bytes 1769480 | tf_op jit(solution)/shard_map/ppermute | solution.py:773
  58.9 6.0 %collective-permute-start.18 = (bf16[4,144,512]{2,1,0:T(8,128)(2,1)S(1)}, bf16[4,144,512]{2,1,0:T(8,128)(2,1)S(1)}, u32[]{:S(2)}, u32[]{:S(2)}) collective-permute-start(bf16[4,144,512]{2,1,0:T(8,128)(2,1)S(1)} %collective-permute-done.14.refs_10_), channel_id=1, source_target_pairs={{0,8},{1,9},{2,10},{3,11},{4,12},{5,13},{6,14},{7,15},{8,0},{9,1},... | collective-permute-start | bytes 1769480 | tf_op jit(solution)/shard_map/ppermute | solution.py:773
  59.0 7.8 %collective-permute-start.17 = (bf16[4,144,512]{2,1,0:T(8,128)(2,1)S(1)}, bf16[4,144,512]{2,1,0:T(8,128)(2,1)}, u32[]{:S(2)}, u32[]{:S(2)}) collective-permute-start(bf16[4,144,512]{2,1,0:T(8,128)(2,1)S(1)} %collective-permute-done.13.refs_9_), channel_id=1, source_target_pairs={{0,8},{1,9},{2,10},{3,11},{4,12},{5,13},{6,14},{7,15},{8,0},{9,1},... | collective-permute-start | bytes 1769480 | tf_op jit(solution)/shard_map/ppermute | solution.py:773
  59.4 3.9 %collective-permute-start.11 = (bf16[4,64,512]{2,1,0:T(8,128)(2,1)S(1)}, bf16[4,64,512]{2,1,0:T(8,128)(2,1)S(1)}, u32[]{:S(2)}, u32[]{:S(2)}) collective-permute-start(bf16[4,64,512]{2,1,0:T(8,128)(2,1)S(1)} %collective-permute-done.7.refs_2_), channel_id=1, source_target_pairs={{0,8},{1,9},{2,10},{3,11},{4,12},{5,13},{6,14},{7,15},{8,0},{9,1},... | collective-permute-start | bytes 786440 | tf_op jit(solution)/shard_map/ppermute | solution.py:773
  63.3 1.5 collective-permute-start.10
  187.8 9.3 %collective-permute-start.24 = (bf16[16,144,512]{2,1,0:T(8,128)(2,1)}, bf16[16,144,512]{2,1,0:T(8,128)(2,1)S(1)}, u32[]{:S(2)}, u32[]{:S(2)}) collective-permute-start(bf16[16,144,512]{2,1,0:T(8,128)(2,1)} %get-tuple-element.53), channel_id=1, source_target_pairs={{0,8},{1,9},{2,10},{3,11},{4,12},{5,13},{6,14},{7,15},{8,0},{9,1},... | collective-permute-start | bytes 7077896 | tf_op jit(solution)/shard_map/ppermute | solution.py:773
  187.9 7.1 %collective-permute-start.20 = (bf16[16,64,512]{2,1,0:T(8,128)(2,1)}, bf16[16,64,512]{2,1,0:T(8,128)(2,1)}, u32[]{:S(2)}, u32[]{:S(2)}) collective-permute-start(bf16[16,64,512]{2,1,0:T(8,128)(2,1)} %get-tuple-element.46), channel_id=1, source_target_pairs={{0,8},{1,9},{2,10},{3,11},{4,12},{5,13},{6,14},{7,15},{8,0},{9,1},... | collective-permute-start | bytes 3145736 | tf_op jit(solution)/shard_map/ppermute | solution.py:773
  197.1 21.8 %collective-permute-start.21 = (bf16[4,64,512]{2,1,0:T(8,128)(2,1)S(1)}, bf16[4,64,512]{2,1,0:T(8,128)(2,1)}, u32[]{:S(2)}, u32[]{:S(2)}) collective-permute-start(bf16[4,64,512]{2,1,0:T(8,128)(2,1)S(1)} %get-tuple-element.73), channel_id=1, source_target_pairs={{0,2},{1,3},{2,0},{3,1},{4,6},{5,7},{6,4},{7,5},{8,10},{9,11},{10,... | collective-permute-start | bytes 786440 | tf_op jit(solution)/shard_map/ppermute | solution.py:773
  199.1 44.1 %collective-permute-start.25 = (bf16[4,144,512]{2,1,0:T(8,128)(2,1)}, bf16[4,144,512]{2,1,0:T(8,128)(2,1)S(1)}, u32[]{:S(2)}, u32[]{:S(2)}) collective-permute-start(bf16[4,144,512]{2,1,0:T(8,128)(2,1)} %get-tuple-element.70), channel_id=1, source_target_pairs={{0,16},{1,17},{2,18},{3,19},{4,20},{5,21},{6,22},{7,23},{8,24},{9,... | collective-permute-start | bytes 1769480 | tf_op jit(solution)/shard_map/ppermute | solution.py:773
  199.6 43.7 %collective-permute-start.27 = (bf16[4,144,512]{2,1,0:T(8,128)(2,1)}, bf16[4,144,512]{2,1,0:T(8,128)(2,1)}, u32[]{:S(2)}, u32[]{:S(2)}) collective-permute-start(bf16[4,144,512]{2,1,0:T(8,128)(2,1)} %get-tuple-element.71), channel_id=1, source_target_pairs={{0,17},{1,16},{2,19},{3,18},{4,21},{5,20},{6,23},{7,22},{8,25},{9,... | collective-permute-start | bytes 1769480 | tf_op jit(solution)/shard_map/ppermute | solution.py:773
  215.6 27.7 %collective-permute-start.26 = (bf16[4,144,512]{2,1,0:T(8,128)(2,1)}, bf16[4,144,512]{2,1,0:T(8,128)(2,1)}, u32[]{:S(2)}, u32[]{:S(2)}) collective-permute-start(bf16[4,144,512]{2,1,0:T(8,128)(2,1)} %get-tuple-element.72), channel_id=1, source_target_pairs={{0,1},{1,0},{2,3},{3,2},{4,5},{5,4},{6,7},{7,6},{8,9},{9,8},{10,11... | collective-permute-start | bytes 1769480 | tf_op jit(solution)/shard_map/ppermute | solution.py:773
  215.6 11.4 %collective-permute-start.23 = (bf16[4,64,512]{2,1,0:T(8,128)(2,1)}, bf16[4,64,512]{2,1,0:T(8,128)(2,1)S(1)}, u32[]{:S(2)}, u32[]{:S(2)}) collective-permute-start(bf16[4,64,512]{2,1,0:T(8,128)(2,1)} %get-tuple-element.74), channel_id=1, source_target_pairs={{0,6},{1,7},{2,4},{3,5},{4,2},{5,3},{6,0},{7,1},{8,14},{9,15},{10,... | collective-permute-start | bytes 786440 | tf_op jit(solution)/shard_map/ppermute | solution.py:773
  219.0 23.1 %collective-permute-start.22 = (bf16[4,64,512]{2,1,0:T(8,128)(2,1)}, bf16[4,64,512]{2,1,0:T(8,128)(2,1)S(1)}, u32[]{:S(2)}, u32[]{:S(2)}) collective-permute-start(bf16[4,64,512]{2,1,0:T(8,128)(2,1)} %get-tuple-element.75), channel_id=1, source_target_pairs={{0,4},{1,5},{2,6},{3,7},{4,0},{5,1},{6,2},{7,3},{8,12},{9,13},{10,... | collective-permute-start | bytes 786440 | tf_op jit(solution)/shard_map/ppermute | solution.py:773
  245.9 6.3 %collective-permute-start.30 = (bf16[64,512]{1,0:T(8,128)(2,1)S(1)}, bf16[64,512]{1,0:T(8,128)(2,1)S(1)}, u32[]{:S(2)}, u32[]{:S(2)}) collective-permute-start(bf16[64,512]{1,0:T(8,128)(2,1)S(1)} %get-tuple-element.79), channel_id=1, source_target_pairs={{0,17},{1,16},{2,19},{3,18},{4,21},{5,20},{6,23},{7,22},{8,25},{9,... | collective-permute-start | bytes 196616 | tf_op jit(solution)/shard_map/ppermute | solution.py:773
  246.9 13.6 %collective-permute-start.29 = (bf16[64,512]{1,0:T(8,128)(2,1)}, bf16[64,512]{1,0:T(8,128)(2,1)}, u32[]{:S(2)}, u32[]{:S(2)}) collective-permute-start(bf16[64,512]{1,0:T(8,128)(2,1)} %get-tuple-element.80), channel_id=1, source_target_pairs={{0,1},{1,0},{2,3},{3,2},{4,5},{5,4},{6,7},{7,6},{8,9},{9,8},{10,11... | collective-permute-start | bytes 196616 | tf_op jit(solution)/shard_map/ppermute | solution.py:773
  247.7 12.8 %collective-permute-start.28 = (bf16[64,512]{1,0:T(8,128)(2,1)}, bf16[64,512]{1,0:T(8,128)(2,1)}, u32[]{:S(2)}, u32[]{:S(2)}) collective-permute-start(bf16[64,512]{1,0:T(8,128)(2,1)} %get-tuple-element.81), channel_id=1, source_target_pairs={{0,16},{1,17},{2,18},{3,19},{4,20},{5,21},{6,22},{7,23},{8,24},{9,... | collective-permute-start | bytes 196616 | tf_op jit(solution)/shard_map/ppermute | solution.py:773
  249.5 11.0 %collective-permute-start.33 = (bf16[144,512]{1,0:T(8,128)(2,1)S(1)}, bf16[144,512]{1,0:T(8,128)(2,1)S(1)}, u32[]{:S(2)}, u32[]{:S(2)}) collective-permute-start(bf16[144,512]{1,0:T(8,128)(2,1)S(1)} %get-tuple-element.76), channel_id=1, source_target_pairs={{0,6},{1,7},{2,4},{3,5},{4,2},{5,3},{6,0},{7,1},{8,14},{9,15},{10,... | collective-permute-start | bytes 442376 | tf_op jit(solution)/shard_map/ppermute | solution.py:773
  252.2 11.5 %collective-permute-start.32 = (bf16[144,512]{1,0:T(8,128)(2,1)S(1)}, bf16[144,512]{1,0:T(8,128)(2,1)}, u32[]{:S(2)}, u32[]{:S(2)}) collective-permute-start(bf16[144,512]{1,0:T(8,128)(2,1)S(1)} %get-tuple-element.77), channel_id=1, source_target_pairs={{0,4},{1,5},{2,6},{3,7},{4,0},{5,1},{6,2},{7,3},{8,12},{9,13},{10,... | collective-permute-start | bytes 442376 | tf_op jit(solution)/shard_map/ppermute | solution.py:773
  252.3 11.5 %collective-permute-start.31 = (bf16[144,512]{1,0:T(8,128)(2,1)S(1)}, bf16[144,512]{1,0:T(8,128)(2,1)}, u32[]{:S(2)}, u32[]{:S(2)}) collective-permute-start(bf16[144,512]{1,0:T(8,128)(2,1)S(1)} %get-tuple-element.78), channel_id=1, source_target_pairs={{0,2},{1,3},{2,0},{3,1},{4,6},{5,7},{6,4},{7,5},{8,10},{9,11},{10,... | collective-permute-start | bytes 442376 | tf_op jit(solution)/shard_map/ppermute | solution.py:773
  260.5 23.5 %copy-start.3 = (f32[98464]{0:T(1024)S(1)}, f32[98464]{0:T(1024)}, u32[]{:S(2)}) copy-start(f32[98464]{0:T(1024)} %param.11) | copy-start | bytes 1181572
  260.5 23.6 %copy-start.13 = (f32[98464]{0:T(1024)S(1)}, f32[98464]{0:T(1024)}, u32[]{:S(2)}) copy-start(f32[98464]{0:T(1024)} %param.12) | copy-start | bytes 1181572
  260.5 23.6 %copy-start.14 = (f32[98464]{0:T(1024)S(1)}, f32[98464]{0:T(1024)}, u32[]{:S(2)}) copy-start(f32[98464]{0:T(1024)} %param.13) | copy-start | bytes 1181572
  267.7 1.2 collective-permute-start.34
  269.6 4.6 %collective-permute-start.37 = (f32[8,128]{1,0:T(8,128)S(1)}, f32[8,128]{1,0:T(8,128)S(1)}, u32[]{:S(2)}, u32[]{:S(2)}) collective-permute-start(f32[8,128]{1,0:T(8,128)S(1)} %broadcast_add_fusion), channel_id=1, source_target_pairs={{0,17},{1,16},{2,19},{3,18},{4,21},{5,20},{6,23},{7,22},{8,25},{9,... | collective-permute-start | bytes 12296 | tf_op jit(solution)/shard_map/ppermute | solution.py:773
  270.5 3.6 %collective-permute-start.36 = (f32[8,128]{1,0:T(8,128)S(1)}, f32[8,128]{1,0:T(8,128)S(1)}, u32[]{:S(2)}, u32[]{:S(2)}) collective-permute-start(f32[8,128]{1,0:T(8,128)S(1)} %broadcast_add_fusion), channel_id=1, source_target_pairs={{0,1},{1,0},{2,3},{3,2},{4,5},{5,4},{6,7},{7,6},{8,9},{9,8},{10,11... | collective-permute-start | bytes 12296 | tf_op jit(solution)/shard_map/ppermute | solution.py:773
  271.5 3.6 %collective-permute-start.35 = (f32[8,128]{1,0:T(8,128)S(1)}, f32[8,128]{1,0:T(8,128)S(1)}, u32[]{:S(2)}, u32[]{:S(2)}) collective-permute-start(f32[8,128]{1,0:T(8,128)S(1)} %broadcast_add_fusion), channel_id=1, source_target_pairs={{0,16},{1,17},{2,18},{3,19},{4,20},{5,21},{6,22},{7,23},{8,24},{9,... | collective-permute-start | bytes 12296 | tf_op jit(solution)/shard_map/ppermute | solution.py:773
  275.7 5.5 %collective-permute-start.40 = (f32[8,128]{1,0:T(8,128)S(1)}, f32[8,128]{1,0:T(8,128)S(1)}, u32[]{:S(2)}, u32[]{:S(2)}) collective-permute-start(f32[8,128]{1,0:T(8,128)S(1)} %add_add_fusion.1), channel_id=1, source_target_pairs={{0,6},{1,7},{2,4},{3,5},{4,2},{5,3},{6,0},{7,1},{8,14},{9,15},{10,... | collective-permute-start | bytes 12296 | tf_op jit(solution)/shard_map/ppermute | solution.py:773
  278.3 4.5 %collective-permute-start.39 = (f32[8,128]{1,0:T(8,128)S(1)}, f32[8,128]{1,0:T(8,128)S(1)}, u32[]{:S(2)}, u32[]{:S(2)}) collective-permute-start(f32[8,128]{1,0:T(8,128)S(1)} %add_add_fusion.1), channel_id=1, source_target_pairs={{0,4},{1,5},{2,6},{3,7},{4,0},{5,1},{6,2},{7,3},{8,12},{9,13},{10,... | collective-permute-start | bytes 12296 | tf_op jit(solution)/shard_map/ppermute | solution.py:773
  278.3 4.5 %collective-permute-start.38 = (f32[8,128]{1,0:T(8,128)S(1)}, f32[8,128]{1,0:T(8,128)S(1)}, u32[]{:S(2)}, u32[]{:S(2)}) collective-permute-start(f32[8,128]{1,0:T(8,128)S(1)} %add_add_fusion.1), channel_id=1, source_target_pairs={{0,2},{1,3},{2,0},{3,1},{4,6},{5,7},{6,4},{7,5},{8,10},{9,11},{10,... | collective-permute-start | bytes 12296 | tf_op jit(solution)/shard_map/ppermute | solution.py:773
  (16 other events, 78.4 us)

commit v2 on v1

--- a/solution.py
+++ b/solution.py
@@ -515,12 +515,12 @@
             normed_low = (hat * vector(2) + vector(3)).astype(bf16)
             normed_grad = jnp.zeros((size, D), f32)
             for j in range(4):
-                down_sum[j] += dot_tn(branch, hidden[hidden_rows(j, start, size), :])
                 slope = hidden[hidden_rows(4 + j, start, size), :].astype(f32)
                 pre_grad = (dot_nt(branch, weight_down(j)) * slope).astype(bf16)
                 add_vector(6 + j, column_sum(pre_grad.astype(f32)))
+                down_sum[j] += dot_tn(branch, hidden[hidden_rows(j, start, size), :])
+                normed_grad = normed_grad + dot_nt(pre_grad, weight_up(j))
                 up_sum[j] += dot_tn(normed_low, pre_grad)
-                normed_grad = normed_grad + dot_nt(pre_grad, weight_up(j))
             add_vector(2, column_sum(normed_grad * hat))
             add_vector(3, column_sum(normed_grad))
             middle_grad = grad + norm_backward(normed_grad, hat, rho, vector(2))
@@ -776,8 +776,7 @@
 def gather_weights(params, device, meanwhile):
     source, _ = row_tables()
     shift = (NPARAM // DEVICES - CHUNK * D) * device
-    edge = jnp.zeros((EXTRA * D,), bf16)
-    line = jnp.concatenate([edge, params.astype(bf16), edge])
+    line = lax.pad(params.astype(bf16), jnp.zeros((), bf16), [(EXTRA * D, EXTRA * D, 0)])
     rows = lax.dynamic_slice(line, (EXTRA * D - shift,), ((CHUNK + EXTRA) * D,)).reshape(CHUNK + EXTRA, D)
     rows = pick_rows(source, device, rows).astype(bf16)
     own_a, own_b = rows[:ROWS_A], rows[ROWS_A:]
@@ -798,6 +797,22 @@
     parts_a = chunks[..., :ROWS_A, :].transpose(1, 2, 3, 0, 4, 5).reshape(8, 4, ROWS_A, D)
     parts_b = chunks[..., ROWS_A:, :].transpose(1, 3, 0, 2, 4, 5).reshape(8, 4, ROWS_B, D)
     return [parts_a[n] for n in range(8)] + [parts_b[n] for n in range(8)]
+
+
+def finish_kernel(shift_ref, wanted_ref, own_a, a_one, a_two, a_three, own_b, b_one, b_two, b_three, rows_out, square_out):
+    part_a = own_a[...] + a_one[...].astype(f32) + a_two[...].astype(f32) + a_three[...].astype(f32)
+    part_b = own_b[...] + b_one[...].astype(f32) + b_two[...].astype(f32) + b_three[...].astype(f32)
+    rows = jnp.concatenate([part_a, part_b], axis=0)
+    pick = jnp.where(wanted_ref[...] == iota((PACKED, PACKED), 1), 1.0, 0.0).astype(bf16)
+    high = rows.astype(bf16)
+    rest = rows - high.astype(f32)
+    middle = rest.astype(bf16)
+    low = (rest - middle.astype(f32)).astype(bf16)
+    rows = dot(pick, high) + dot(pick, middle) + dot(pick, low)
+    rows_out[...] = rows
+    index = iota((PACKED, D), 0) * D + iota((PACKED, D), 1) - shift_ref[0]
+    own = (index >= 0) & (index < NPARAM // DEVICES)
+    square_out[...] = jnp.full((8, 128), jnp.sum(jnp.where(own, rows * rows, 0.0)), f32)
 
 
 def reduce_grads(parts, device, place, final_states, input_grad):
@@ -817,15 +832,20 @@
     got_a = [send(line_a[n].astype(bf16), *PLANE[n]) for n in (1, 2, 3)]
     input_grad = restore(place, input_grad, "restore_grad")
     got_a, got_b, input_grad = lax.optimization_barrier((got_a, got_b, input_grad))
-    own_a = sum((part.astype(f32) for part in got_a), line_a[0])
-    own_b = sum((part.astype(f32) for part in got_b), plane_b[0])
-    rows = pick_rows(target, device, jnp.concatenate([own_a, own_b], axis=0), lax.Precision.HIGHEST)
     shift = (NPARAM // DEVICES - CHUNK * D) * device
-    return lax.dynamic_slice(rows.reshape(-1), (shift,), (NPARAM // DEVICES,)), final_states, input_grad
+    wanted = lax.dynamic_slice(jnp.asarray(target), (device, 0), (1, PACKED)).reshape(PACKED, 1)
+    rows, square_sum = pl.pallas_call(
+        finish_kernel,
+        out_shape=(shape_of(PACKED, D), shape_of(8, 128)),
+        in_specs=[pl.BlockSpec(memory_space=pltpu.SMEM)] + [pl.BlockSpec(memory_space=pltpu.VMEM)] * 9,
+        out_specs=(pl.BlockSpec(memory_space=pltpu.VMEM),) * 2,
+        name="finish",
+    )(shift.astype(i32).reshape(1), wanted, line_a[0], *got_a, plane_b[0], *got_b)
+    reduced = lax.dynamic_slice(rows.reshape(-1), (shift,), (NPARAM // DEVICES,))
+    return reduced, sum_all(square_sum), final_states, input_grad
 
 
 def sum_all(value):
-    value = jnp.broadcast_to(value, (8, 128))
     value = value + send(value, dc=1)
     value = value + sum(send(value, dy, dx) for dy, dx in PLANE[1:])
     return (value + sum(send(value, dz=dz) for dz in (1, 2, 3)))[0, 0]
@@ -860,8 +880,7 @@
     place, sorted_states, sorted_cotangent, meta = prepared
     final_states, input_grad, parts = layer(meta, sorted_states, sorted_cotangent, pieces)
     if blockwise:
-        reduced, final_states, input_grad = reduce_grads(parts, device, place, final_states, input_grad)
-        square_sum = sum_all(jnp.sum(reduced * reduced))
+        reduced, square_sum, final_states, input_grad = reduce_grads(parts, device, place, final_states, input_grad)
     else:
         final_states = restore(place, final_states, "restore_final")
         input_grad = restore(place, input_grad, "restore_grad")

time: 289 us -> 282 us (0.976)
  Pallas kernels: 140 us -> 127 us
  starting transfers between devices: 67.6 us -> 76.3 us
  other arithmetic: 15 us -> 11.6 us
    pallas_call x1, Pallas kernels: 121 us -> 106 us  [layer(): pl.pallas_call(layer_kernel, out_shape=(shape_of(SEQ, D), shape_of(SEQ, D...]
    ppermute x41, starting transfers between devices: 67.6 us -> 76.3 us  [send(): return lax.ppermute(array, ('dp', 'fsdp'), pairs)]
  transfers between devices with their start and end apart: 41 -> 41, of which waited for: 14 -> 18; matrix products, arithmetic and copies ran while one was open for 2% -> 3% of each run, Pallas kernels for 7% -> 4%
where the time goes in v2:
time: 282 us; the launch traced here: 281 us
  Pallas kernels  127 us (45%)
  starting transfers between devices  76.3 us (27%)
  waiting for transfers between devices  52.7 us (19%)
  other arithmetic  11.6 us (4%)
  local copies, waits for them, and re-layouts  8.87 us (3%)
  between operations  3.62 us (1%)
    pallas_call x1, Pallas kernels, layer(): pl.pallas_call(layer_kernel, out_shape=(shape_of(SEQ, D), shape_of(SEQ, D...  106 us
    ppermute x41, starting transfers between devices, send(): return lax.ppermute(array, ('dp', 'fsdp'), pairs)  76.3 us
    ppermute x41, waiting for transfers between devices, send(): return lax.ppermute(array, ('dp', 'fsdp'), pairs)  52.7 us
    pallas_call x2, Pallas kernels, restore(): pl.pallas_call(restore_kernel, out_shape=jax.ShapeDtypeStruct((SEQ, D), f...  13.1 us
    pallas_call x1, Pallas kernels, prepare(): pl.pallas_call(prepare_kernel, out_shape=(jax.ShapeDtypeStruct((8, SEQ),...  5.81 us
  transfers between devices with their start and end apart: 41, of which 18 were waited for; matrix products, arithmetic and copies ran while one was open for 3% of the time, Pallas kernels for 4%

profile of v2, /device:TPU:0, one launch (start us, length us, event | category | flops | bytes accessed | tf_op | source)
XLA Modules:
  0.0 280.6 jit_solution(17541969572462713139)
XLA Ops:
  0.7 1.0 convert_element_type.58
  3.1 3.1 %collective-permute-start.3 = (bf16[144,512]{1,0:T(8,128)(2,1)S(1)}, bf16[144,512]{1,0:T(8,128)(2,1)S(1)}, u32[]{:S(2)}, u32[]{:S(2)}) collective-permute-start(bf16[144,512]{1,0:T(8,128)(2,1)S(1)} %get-tuple-element.87), channel_id=1, source_target_pairs={{0,2},{1,3},{2,0},{3,1},{4,6},{5,7},{6,4},{7,5},{8,10},{9,11},{10,... | collective-permute-start | bytes 442376 | tf_op jit(solution)/shard_map/ppermute | solution.py:773
  6.1 2.6 collective-permute-start.4
  8.7 1.8 collective-permute-start
  10.6 1.5 collective-permute-start.1
  13.3 2.4 collective-permute-start.2
  15.7 5.8 %prepare.1 = (f32[8,1024]{1,0:T(8,128)}, bf16[1024,512]{1,0:T(8,128)(2,1)}, bf16[1024,512]{1,0:T(8,128)(2,1)}, s32[6]{0:T(128)}) custom-call(s32[1]{0:T(128)S(6)} %copy.21.length_ref, s32[4]{0:T(128)} %pad_add_fusion.index_ref, s32[1,1024]{1,0:T(1,128)} %count_ref.1, bf16[1024,512]{1,0:T(8,128)(2,1)} %bitcast.52, bf16[1024,512]{1,0:T(8,128)(2,1)} %bitcast.53), custom_call_target="tpu_custom_call" | custom-call | flops 6000000000 | bytes 4000000 | tf_op jit(solution)/shard_map/prepare/pallas_call | solution.py:140
  22.6 1.5 collective-permute-start.13
  24.1 1.5 collective-permute-start.14
  26.1 3.4 %collective-permute-start.7 = (bf16[4,64,512]{2,1,0:T(8,128)(2,1)S(1)}, bf16[4,64,512]{2,1,0:T(8,128)(2,1)S(1)}, u32[]{:S(2)}, u32[]{:S(2)}) collective-permute-start(bf16[4,64,512]{2,1,0:T(8,128)(2,1)S(1)} %pad_maximum_fusion.1.refs_0_), channel_id=1, source_target_pairs={{0,4},{1,5},{2,6},{3,7},{4,0},{5,1},{6,2},{7,3},{8,12},{9,13},{10,... | collective-permute-start | bytes 786440 | tf_op jit(solution)/shard_map/ppermute | solution.py:773
  29.7 3.7 %collective-permute-start.8 = (bf16[4,64,512]{2,1,0:T(8,128)(2,1)S(1)}, bf16[4,64,512]{2,1,0:T(8,128)(2,1)S(1)}, u32[]{:S(2)}, u32[]{:S(2)}) collective-permute-start(bf16[4,64,512]{2,1,0:T(8,128)(2,1)S(1)} %pad_maximum_fusion.1.refs_0_), channel_id=1, source_target_pairs={{0,6},{1,7},{2,4},{3,5},{4,2},{5,3},{6,0},{7,1},{8,14},{9,15},{10,... | collective-permute-start | bytes 786440 | tf_op jit(solution)/shard_map/ppermute | solution.py:773
  33.4 12.8 %collective-permute-done.7.refs_2_ = bf16[4,64,512]{2,1,0:T(8,128)(2,1)S(1)} collective-permute-done((bf16[4,64,512]{2,1,0:T(8,128)(2,1)S(1)}, bf16[4,64,512]{2,1,0:T(8,128)(2,1)S(1)}, u32[]{:S(2)}, u32[]{:S(2)}) %collective-permute-start.7) | collective-permute-done | bytes 262176 | tf_op jit(solution)/shard_map/ppermute | solution.py:773
  46.8 1.2 collective-permute-done.9.refs_4_
  48.6 1.5 collective-permute-done.15.refs_11_
  50.6 2.0 collective-permute-done.11.refs_6_
  53.0 1.2 collective-permute-done.12.refs_7_
  56.1 105.8 %layer.1 = (f32[1024,512]{1,0:T(8,128)}, f32[1024,512]{1,0:T(8,128)}, bf16[16,64,512]{2,1,0:T(8,128)(2,1)}, bf16[16,64,512]{2,1,0:T(8,128)(2,1)}, bf16[16,144,51...) custom-call(s32[6]{0:T(128)} %get-tuple-element.43.meta, ...), custom_call_target="tpu_custom_call" | custom-call | tf_op jit(solution)/shard_map/layer/pallas_call | solution.py:671
  161.9 27.7 %collective-permute-start.24 = (bf16[16,144,512]{2,1,0:T(8,128)(2,1)}, bf16[16,144,512]{2,1,0:T(8,128)(2,1)S(1)}, u32[]{:S(2)}, u32[]{:S(2)}) collective-permute-start(bf16[16,144,512]{2,1,0:T(8,128)(2,1)} %get-tuple-element.55), channel_id=1, source_target_pairs={{0,8},{1,9},{2,10},{3,11},{4,12},{5,13},{6,14},{7,15},{8,0},{9,1},... | collective-permute-start | bytes 7077896 | tf_op jit(solution)/shard_map/ppermute | solution.py:773
  189.7 6.6 %restore_final.1 = f32[1024,512]{1,0:T(8,128)} custom-call(f32[8,1024]{1,0:T(8,128)} %get-tuple-element.49.place_ref, f32[1024,512]{1,0:T(8,128)} %get-tuple-element.50.sorted_ref), custom_call_target="tpu_custom_call" | custom-call | flops 6000000000 | bytes 4000000 | tf_op jit(solution)/shard_map/restore_final/pallas_call | solution.py:187
  196.3 2.1 slice_add_fusion.6
  198.5 1.4 slice_add_fusion.2
  200.4 3.5 %collective-permute-start.27 = (bf16[4,144,512]{2,1,0:T(8,128)(2,1)}, bf16[4,144,512]{2,1,0:T(8,128)(2,1)}, u32[]{:S(2)}, u32[]{:S(2)}) collective-permute-start(bf16[4,144,512]{2,1,0:T(8,128)(2,1)} %get-tuple-element.75), channel_id=1, source_target_pairs={{0,17},{1,16},{2,19},{3,18},{4,21},{5,20},{6,23},{7,22},{8,25},{9,... | collective-permute-start | bytes 1769480 | tf_op jit(solution)/shard_map/ppermute | solution.py:773
  203.9 2.7 collective-permute-start.22
  207.2 1.1 collective-permute-start.23
  209.8 15.6 %collective-permute-done.22 = bf16[4,64,512]{2,1,0:T(8,128)(2,1)S(1)} collective-permute-done((bf16[4,64,512]{2,1,0:T(8,128)(2,1)}, bf16[4,64,512]{2,1,0:T(8,128)(2,1)S(1)}, u32[]{:S(2)}, u32[]{:S(2)}) %collective-permute-start.22) | collective-permute-done | bytes 262176 | tf_op jit(solution)/shard_map/ppermute | solution.py:773
  225.4 1.2 convert_add_fusion.1
  226.6 3.6 %collective-permute-done.27 = bf16[4,144,512]{2,1,0:T(8,128)(2,1)} collective-permute-done((bf16[4,144,512]{2,1,0:T(8,128)(2,1)}, bf16[4,144,512]{2,1,0:T(8,128)(2,1)}, u32[]{:S(2)}, u32[]{:S(2)}) %collective-permute-start.27) | collective-permute-done | bytes 589856 | tf_op jit(solution)/shard_map/ppermute | solution.py:773
  230.2 2.0 convert_add_fusion
  232.2 6.5 %restore_grad.1 = f32[1024,512]{1,0:T(8,128)} custom-call(f32[8,1024]{1,0:T(8,128)} %get-tuple-element.49.place_ref, f32[1024,512]{1,0:T(8,128)} %get-tuple-element.59.sorted_ref), custom_call_target="tpu_custom_call" | custom-call | flops 6000000000 | bytes 4000000 | tf_op jit(solution)/shard_map/restore_grad/pallas_call | solution.py:187
  240.0 2.1 collective-permute-start.31
  242.1 1.7 collective-permute-start.32
  243.8 1.2 collective-permute-start.33
  245.0 1.7 collective-permute-start.29
  248.3 1.0 collective-permute-done.29.a_two
  249.2 2.6 collective-permute-done.30.a_three
  251.9 3.5 %collective-permute-done.32.b_two = bf16[144,512]{1,0:T(8,128)(2,1)S(1)} collective-permute-done((bf16[144,512]{1,0:T(8,128)(2,1)S(1)}, bf16[144,512]{1,0:T(8,128)(2,1)S(1)}, u32[]{:S(2)}, u32[]{:S(2)}) %collective-permute-start.32) | collective-permute-done | bytes 147488 | tf_op jit(solution)/shard_map/ppermute | solution.py:773
  256.1 2.5 finish.1
  258.6 1.4 collective-permute-done.34
  260.7 1.1 collective-permute-start.35
  261.7 1.0 collective-permute-start.36
  262.7 1.5 collective-permute-start.37
  264.3 1.1 collective-permute-done.36
  265.3 1.9 collective-permute-done.37
  267.2 2.6 collective-permute-start.38
  270.4 1.8 collective-permute-start.40
  272.2 1.2 copy.20
  274.3 1.5 collective-permute-done.40
  277.1 1.5 fusion.2
  (124 shorter events, 17.6 us)
Async XLA Ops:
  3.1 18.6 %collective-permute-start.3 = (bf16[144,512]{1,0:T(8,128)(2,1)S(1)}, bf16[144,512]{1,0:T(8,128)(2,1)S(1)}, u32[]{:S(2)}, u32[]{:S(2)}) collective-permute-start(bf16[144,512]{1,0:T(8,128)(2,1)S(1)} %get-tuple-element.87), channel_id=1, source_target_pairs={{0,2},{1,3},{2,0},{3,1},{4,6},{5,7},{6,4},{7,5},{8,10},{9,11},{10,... | collective-permute-start | bytes 442376 | tf_op jit(solution)/shard_map/ppermute | solution.py:773
  6.1 15.5 %collective-permute-start.4 = (bf16[144,512]{1,0:T(8,128)(2,1)S(1)}, bf16[144,512]{1,0:T(8,128)(2,1)S(1)}, u32[]{:S(2)}, u32[]{:S(2)}) collective-permute-start(bf16[144,512]{1,0:T(8,128)(2,1)S(1)} %get-tuple-element.87), channel_id=1, source_target_pairs={{0,4},{1,5},{2,6},{3,7},{4,0},{5,1},{6,2},{7,3},{8,12},{9,13},{10,... | collective-permute-start | bytes 442376 | tf_op jit(solution)/shard_map/ppermute | solution.py:773
  8.7 12.9 %collective-permute-start.5 = (bf16[144,512]{1,0:T(8,128)(2,1)S(1)}, bf16[144,512]{1,0:T(8,128)(2,1)S(1)}, u32[]{:S(2)}, u32[]{:S(2)}) collective-permute-start(bf16[144,512]{1,0:T(8,128)(2,1)S(1)} %get-tuple-element.87), channel_id=1, source_target_pairs={{0,6},{1,7},{2,4},{3,5},{4,2},{5,3},{6,0},{7,1},{8,14},{9,15},{10,... | collective-permute-start | bytes 442376 | tf_op jit(solution)/shard_map/ppermute | solution.py:773
  8.7 4.5 %collective-permute-start = (bf16[64,512]{1,0:T(8,128)(2,1)S(1)}, bf16[64,512]{1,0:T(8,128)(2,1)S(1)}, u32[]{:S(2)}, u32[]{:S(2)}) collective-permute-start(bf16[64,512]{1,0:T(8,128)(2,1)S(1)} %get-tuple-element.89), channel_id=1, source_target_pairs={{0,16},{1,17},{2,18},{3,19},{4,20},{5,21},{6,22},{7,23},{8,24},{9,... | collective-permute-start | bytes 196616 | tf_op jit(solution)/shard_map/ppermute | solution.py:773
  10.6 11.0 %collective-permute-start.1 = (bf16[64,512]{1,0:T(8,128)(2,1)S(1)}, bf16[64,512]{1,0:T(8,128)(2,1)S(1)}, u32[]{:S(2)}, u32[]{:S(2)}) collective-permute-start(bf16[64,512]{1,0:T(8,128)(2,1)S(1)} %get-tuple-element.89), channel_id=1, source_target_pairs={{0,1},{1,0},{2,3},{3,2},{4,5},{5,4},{6,7},{7,6},{8,9},{9,8},{10,11... | collective-permute-start | bytes 196616 | tf_op jit(solution)/shard_map/ppermute | solution.py:773
  13.3 8.3 %collective-permute-start.2 = (bf16[64,512]{1,0:T(8,128)(2,1)S(1)}, bf16[64,512]{1,0:T(8,128)(2,1)S(1)}, u32[]{:S(2)}, u32[]{:S(2)}) collective-permute-start(bf16[64,512]{1,0:T(8,128)(2,1)S(1)} %get-tuple-element.89), channel_id=1, source_target_pairs={{0,17},{1,16},{2,19},{3,18},{4,21},{5,20},{6,23},{7,22},{8,25},{9,... | collective-permute-start | bytes 196616 | tf_op jit(solution)/shard_map/ppermute | solution.py:773
  21.6 34.5 %copy-start.5 = (bf16[4,64,512]{2,1,0:T(8,128)(2,1)}, bf16[4,64,512]{2,1,0:T(8,128)(2,1)S(1)}, u32[]{:S(2)}) copy-start(bf16[4,64,512]{2,1,0:T(8,128)(2,1)S(1)} %pad_maximum_fusion.1.refs_0_) | copy-start | bytes 786436
  21.8 34.4 %copy-start = (bf16[4,144,512]{2,1,0:T(8,128)(2,1)}, bf16[4,144,512]{2,1,0:T(8,128)(2,1)S(1)}, u32[]{:S(2)}) copy-start(bf16[4,144,512]{2,1,0:T(8,128)(2,1)S(1)} %pad_maximum_fusion.refs_8_) | copy-start | bytes 1769476
  21.8 8.0 %collective-permute-start.6 = (bf16[4,64,512]{2,1,0:T(8,128)(2,1)S(1)}, bf16[4,64,512]{2,1,0:T(8,128)(2,1)S(1)}, u32[]{:S(2)}, u32[]{:S(2)}) collective-permute-start(bf16[4,64,512]{2,1,0:T(8,128)(2,1)S(1)} %pad_maximum_fusion.1.refs_0_), channel_id=1, source_target_pairs={{0,2},{1,3},{2,0},{3,1},{4,6},{5,7},{6,4},{7,5},{8,10},{9,11},{10,... | collective-permute-start | bytes 786440 | tf_op jit(solution)/shard_map/ppermute | solution.py:773
  22.6 25.4 %collective-permute-start.13 = (bf16[4,144,512]{2,1,0:T(8,128)(2,1)S(1)}, bf16[4,144,512]{2,1,0:T(8,128)(2,1)S(1)}, u32[]{:S(2)}, u32[]{:S(2)}) collective-permute-start(bf16[4,144,512]{2,1,0:T(8,128)(2,1)S(1)} %pad_maximum_fusion.refs_8_), channel_id=1, source_target_pairs={{0,16},{1,17},{2,18},{3,19},{4,20},{5,21},{6,22},{7,23},{8,24},{9,... | collective-permute-start | bytes 1769480 | tf_op jit(solution)/shard_map/ppermute | solution.py:773
  24.1 24.3 %collective-permute-start.14 = (bf16[4,144,512]{2,1,0:T(8,128)(2,1)S(1)}, bf16[4,144,512]{2,1,0:T(8,128)(2,1)S(1)}, u32[]{:S(2)}, u32[]{:S(2)}) collective-permute-start(bf16[4,144,512]{2,1,0:T(8,128)(2,1)S(1)} %pad_maximum_fusion.refs_8_), channel_id=1, source_target_pairs={{0,1},{1,0},{2,3},{3,2},{4,5},{5,4},{6,7},{7,6},{8,9},{9,8},{10,11... | collective-permute-start | bytes 1769480 | tf_op jit(solution)/shard_map/ppermute | solution.py:773
  25.6 24.5 %collective-permute-start.15 = (bf16[4,144,512]{2,1,0:T(8,128)(2,1)S(1)}, bf16[4,144,512]{2,1,0:T(8,128)(2,1)S(1)}, u32[]{:S(2)}, u32[]{:S(2)}) collective-permute-start(bf16[4,144,512]{2,1,0:T(8,128)(2,1)S(1)} %pad_maximum_fusion.refs_8_), channel_id=1, source_target_pairs={{0,17},{1,16},{2,19},{3,18},{4,21},{5,20},{6,23},{7,22},{8,25},{9,... | collective-permute-start | bytes 1769480 | tf_op jit(solution)/shard_map/ppermute | solution.py:773
  26.1 20.1 %collective-permute-start.7 = (bf16[4,64,512]{2,1,0:T(8,128)(2,1)S(1)}, bf16[4,64,512]{2,1,0:T(8,128)(2,1)S(1)}, u32[]{:S(2)}, u32[]{:S(2)}) collective-permute-start(bf16[4,64,512]{2,1,0:T(8,128)(2,1)S(1)} %pad_maximum_fusion.1.refs_0_), channel_id=1, source_target_pairs={{0,4},{1,5},{2,6},{3,7},{4,0},{5,1},{6,2},{7,3},{8,12},{9,13},{10,... | collective-permute-start | bytes 786440 | tf_op jit(solution)/shard_map/ppermute | solution.py:773
  29.7 24.5 %copy-start.16 = (bf16[4,64,512]{2,1,0:T(8,128)(2,1)}, bf16[4,64,512]{2,1,0:T(8,128)(2,1)S(1)}, u32[]{:S(2)}) copy-start(bf16[4,64,512]{2,1,0:T(8,128)(2,1)S(1)} %collective-permute-done.6.refs_1_) | copy-start | bytes 786436
  29.7 16.5 %collective-permute-start.8 = (bf16[4,64,512]{2,1,0:T(8,128)(2,1)S(1)}, bf16[4,64,512]{2,1,0:T(8,128)(2,1)S(1)}, u32[]{:S(2)}, u32[]{:S(2)}) collective-permute-start(bf16[4,64,512]{2,1,0:T(8,128)(2,1)S(1)} %pad_maximum_fusion.1.refs_0_), channel_id=1, source_target_pairs={{0,6},{1,7},{2,4},{3,5},{4,2},{5,3},{6,0},{7,1},{8,14},{9,15},{10,... | collective-permute-start | bytes 786440 | tf_op jit(solution)/shard_map/ppermute | solution.py:773
  46.2 1.7 collective-permute-start.9
  46.3 3.8 %collective-permute-start.10 = (bf16[4,64,512]{2,1,0:T(8,128)(2,1)S(1)}, bf16[4,64,512]{2,1,0:T(8,128)(2,1)S(1)}, u32[]{:S(2)}, u32[]{:S(2)}) collective-permute-start(bf16[4,64,512]{2,1,0:T(8,128)(2,1)S(1)} %collective-permute-done.6.refs_1_), channel_id=1, source_target_pairs={{0,8},{1,9},{2,10},{3,11},{4,12},{5,13},{6,14},{7,15},{8,0},{9,1},... | collective-permute-start | bytes 786440 | tf_op jit(solution)/shard_map/ppermute | solution.py:773
  47.9 6.2 %collective-permute-start.16 = (bf16[4,144,512]{2,1,0:T(8,128)(2,1)S(1)}, bf16[4,144,512]{2,1,0:T(8,128)(2,1)S(1)}, u32[]{:S(2)}, u32[]{:S(2)}) collective-permute-start(bf16[4,144,512]{2,1,0:T(8,128)(2,1)S(1)} %pad_maximum_fusion.refs_8_), channel_id=1, source_target_pairs={{0,8},{1,9},{2,10},{3,11},{4,12},{5,13},{6,14},{7,15},{8,0},{9,1},... | collective-permute-start | bytes 1769480 | tf_op jit(solution)/shard_map/ppermute | solution.py:773
  48.0 6.1 %collective-permute-start.17 = (bf16[4,144,512]{2,1,0:T(8,128)(2,1)S(1)}, bf16[4,144,512]{2,1,0:T(8,128)(2,1)S(1)}, u32[]{:S(2)}, u32[]{:S(2)}) collective-permute-start(bf16[4,144,512]{2,1,0:T(8,128)(2,1)S(1)} %collective-permute-done.13.refs_9_), channel_id=1, source_target_pairs={{0,8},{1,9},{2,10},{3,11},{4,12},{5,13},{6,14},{7,15},{8,0},{9,1},... | collective-permute-start | bytes 1769480 | tf_op jit(solution)/shard_map/ppermute | solution.py:773
  48.4 5.7 %collective-permute-start.18 = (bf16[4,144,512]{2,1,0:T(8,128)(2,1)S(1)}, bf16[4,144,512]{2,1,0:T(8,128)(2,1)S(1)}, u32[]{:S(2)}, u32[]{:S(2)}) collective-permute-start(bf16[4,144,512]{2,1,0:T(8,128)(2,1)S(1)} %collective-permute-done.14.refs_10_), channel_id=1, source_target_pairs={{0,8},{1,9},{2,10},{3,11},{4,12},{5,13},{6,14},{7,15},{8,0},{9,1},... | collective-permute-start | bytes 1769480 | tf_op jit(solution)/shard_map/ppermute | solution.py:773
  50.1 6.0 %collective-permute-start.19 = (bf16[4,144,512]{2,1,0:T(8,128)(2,1)S(1)}, bf16[4,144,512]{2,1,0:T(8,128)(2,1)}, u32[]{:S(2)}, u32[]{:S(2)}) collective-permute-start(bf16[4,144,512]{2,1,0:T(8,128)(2,1)S(1)} %collective-permute-done.15.refs_11_), channel_id=1, source_target_pairs={{0,8},{1,9},{2,10},{3,11},{4,12},{5,13},{6,14},{7,15},{8,0},{9,1},... | collective-permute-start | bytes 1769480 | tf_op jit(solution)/shard_map/ppermute | solution.py:773
  50.1 2.5 collective-permute-start.11
  52.6 1.5 collective-permute-start.12
  161.9 36.5 %collective-permute-start.24 = (bf16[16,144,512]{2,1,0:T(8,128)(2,1)}, bf16[16,144,512]{2,1,0:T(8,128)(2,1)S(1)}, u32[]{:S(2)}, u32[]{:S(2)}) collective-permute-start(bf16[16,144,512]{2,1,0:T(8,128)(2,1)} %get-tuple-element.55), channel_id=1, source_target_pairs={{0,8},{1,9},{2,10},{3,11},{4,12},{5,13},{6,14},{7,15},{8,0},{9,1},... | collective-permute-start | bytes 7077896 | tf_op jit(solution)/shard_map/ppermute | solution.py:773
  189.6 6.7 %collective-permute-start.20 = (bf16[16,64,512]{2,1,0:T(8,128)(2,1)}, bf16[16,64,512]{2,1,0:T(8,128)(2,1)}, u32[]{:S(2)}, u32[]{:S(2)}) collective-permute-start(bf16[16,64,512]{2,1,0:T(8,128)(2,1)} %get-tuple-element.48), channel_id=1, source_target_pairs={{0,8},{1,9},{2,10},{3,11},{4,12},{5,13},{6,14},{7,15},{8,0},{9,1},... | collective-permute-start | bytes 3145736 | tf_op jit(solution)/shard_map/ppermute | solution.py:773
  198.4 8.8 %collective-permute-start.21 = (bf16[4,64,512]{2,1,0:T(8,128)(2,1)S(1)}, bf16[4,64,512]{2,1,0:T(8,128)(2,1)}, u32[]{:S(2)}, u32[]{:S(2)}) collective-permute-start(bf16[4,64,512]{2,1,0:T(8,128)(2,1)S(1)} %get-tuple-element.77), channel_id=1, source_target_pairs={{0,2},{1,3},{2,0},{3,1},{4,6},{5,7},{6,4},{7,5},{8,10},{9,11},{10,... | collective-permute-start | bytes 786440 | tf_op jit(solution)/shard_map/ppermute | solution.py:773
  200.4 26.2 %collective-permute-start.25 = (bf16[4,144,512]{2,1,0:T(8,128)(2,1)}, bf16[4,144,512]{2,1,0:T(8,128)(2,1)S(1)}, u32[]{:S(2)}, u32[]{:S(2)}) collective-permute-start(bf16[4,144,512]{2,1,0:T(8,128)(2,1)} %get-tuple-element.74), channel_id=1, source_target_pairs={{0,16},{1,17},{2,18},{3,19},{4,20},{5,21},{6,22},{7,23},{8,24},{9,... | collective-permute-start | bytes 1769480 | tf_op jit(solution)/shard_map/ppermute | solution.py:773
  200.4 26.2 %collective-permute-start.26 = (bf16[4,144,512]{2,1,0:T(8,128)(2,1)}, bf16[4,144,512]{2,1,0:T(8,128)(2,1)}, u32[]{:S(2)}, u32[]{:S(2)}) collective-permute-start(bf16[4,144,512]{2,1,0:T(8,128)(2,1)} %get-tuple-element.76), channel_id=1, source_target_pairs={{0,1},{1,0},{2,3},{3,2},{4,5},{5,4},{6,7},{7,6},{8,9},{9,8},{10,11... | collective-permute-start | bytes 1769480 | tf_op jit(solution)/shard_map/ppermute | solution.py:773
  200.4 29.8 %collective-permute-start.27 = (bf16[4,144,512]{2,1,0:T(8,128)(2,1)}, bf16[4,144,512]{2,1,0:T(8,128)(2,1)}, u32[]{:S(2)}, u32[]{:S(2)}) collective-permute-start(bf16[4,144,512]{2,1,0:T(8,128)(2,1)} %get-tuple-element.75), channel_id=1, source_target_pairs={{0,17},{1,16},{2,19},{3,18},{4,21},{5,20},{6,23},{7,22},{8,25},{9,... | collective-permute-start | bytes 1769480 | tf_op jit(solution)/shard_map/ppermute | solution.py:773
  203.9 21.5 %collective-permute-start.22 = (bf16[4,64,512]{2,1,0:T(8,128)(2,1)}, bf16[4,64,512]{2,1,0:T(8,128)(2,1)S(1)}, u32[]{:S(2)}, u32[]{:S(2)}) collective-permute-start(bf16[4,64,512]{2,1,0:T(8,128)(2,1)} %get-tuple-element.79), channel_id=1, source_target_pairs={{0,4},{1,5},{2,6},{3,7},{4,0},{5,1},{6,2},{7,3},{8,12},{9,13},{10,... | collective-permute-start | bytes 786440 | tf_op jit(solution)/shard_map/ppermute | solution.py:773
  207.2 18.2 %collective-permute-start.23 = (bf16[4,64,512]{2,1,0:T(8,128)(2,1)}, bf16[4,64,512]{2,1,0:T(8,128)(2,1)S(1)}, u32[]{:S(2)}, u32[]{:S(2)}) collective-permute-start(bf16[4,64,512]{2,1,0:T(8,128)(2,1)} %get-tuple-element.78), channel_id=1, source_target_pairs={{0,6},{1,7},{2,4},{3,5},{4,2},{5,3},{6,0},{7,1},{8,14},{9,15},{10,... | collective-permute-start | bytes 786440 | tf_op jit(solution)/shard_map/ppermute | solution.py:773
  238.8 38.2 %copy-start.3 = (f32[98464]{0:T(1024)S(1)}, f32[98464]{0:T(1024)}, u32[]{:S(2)}) copy-start(f32[98464]{0:T(1024)} %param.11) | copy-start | bytes 1181572
  238.8 38.2 %copy-start.13 = (f32[98464]{0:T(1024)S(1)}, f32[98464]{0:T(1024)}, u32[]{:S(2)}) copy-start(f32[98464]{0:T(1024)} %param.12) | copy-start | bytes 1181572
  238.8 38.2 %copy-start.14 = (f32[98464]{0:T(1024)S(1)}, f32[98464]{0:T(1024)}, u32[]{:S(2)}) copy-start(f32[98464]{0:T(1024)} %param.13) | copy-start | bytes 1181572
  238.9 7.8 %collective-permute-start.28 = (bf16[64,512]{1,0:T(8,128)(2,1)S(1)}, bf16[64,512]{1,0:T(8,128)(2,1)S(1)}, u32[]{:S(2)}, u32[]{:S(2)}) collective-permute-start(bf16[64,512]{1,0:T(8,128)(2,1)S(1)} %get-tuple-element.85), channel_id=1, source_target_pairs={{0,16},{1,17},{2,18},{3,19},{4,20},{5,21},{6,22},{7,23},{8,24},{9,... | collective-permute-start | bytes 196616 | tf_op jit(solution)/shard_map/ppermute | solution.py:773
  240.0 11.9 %collective-permute-start.31 = (bf16[144,512]{1,0:T(8,128)(2,1)S(1)}, bf16[144,512]{1,0:T(8,128)(2,1)S(1)}, u32[]{:S(2)}, u32[]{:S(2)}) collective-permute-start(bf16[144,512]{1,0:T(8,128)(2,1)S(1)} %get-tuple-element.82), channel_id=1, source_target_pairs={{0,2},{1,3},{2,0},{3,1},{4,6},{5,7},{6,4},{7,5},{8,10},{9,11},{10,... | collective-permute-start | bytes 442376 | tf_op jit(solution)/shard_map/ppermute | solution.py:773
  242.1 13.3 %collective-permute-start.32 = (bf16[144,512]{1,0:T(8,128)(2,1)S(1)}, bf16[144,512]{1,0:T(8,128)(2,1)S(1)}, u32[]{:S(2)}, u32[]{:S(2)}) collective-permute-start(bf16[144,512]{1,0:T(8,128)(2,1)S(1)} %get-tuple-element.81), channel_id=1, source_target_pairs={{0,4},{1,5},{2,6},{3,7},{4,0},{5,1},{6,2},{7,3},{8,12},{9,13},{10,... | collective-permute-start | bytes 442376 | tf_op jit(solution)/shard_map/ppermute | solution.py:773
  243.8 11.6 %collective-permute-start.33 = (bf16[144,512]{1,0:T(8,128)(2,1)S(1)}, bf16[144,512]{1,0:T(8,128)(2,1)S(1)}, u32[]{:S(2)}, u32[]{:S(2)}) collective-permute-start(bf16[144,512]{1,0:T(8,128)(2,1)S(1)} %get-tuple-element.80), channel_id=1, source_target_pairs={{0,6},{1,7},{2,4},{3,5},{4,2},{5,3},{6,0},{7,1},{8,14},{9,15},{10,... | collective-permute-start | bytes 442376 | tf_op jit(solution)/shard_map/ppermute | solution.py:773
  245.0 4.3 %collective-permute-start.29 = (bf16[64,512]{1,0:T(8,128)(2,1)S(1)}, bf16[64,512]{1,0:T(8,128)(2,1)S(1)}, u32[]{:S(2)}, u32[]{:S(2)}) collective-permute-start(bf16[64,512]{1,0:T(8,128)(2,1)S(1)} %get-tuple-element.84), channel_id=1, source_target_pairs={{0,1},{1,0},{2,3},{3,2},{4,5},{5,4},{6,7},{7,6},{8,9},{9,8},{10,11... | collective-permute-start | bytes 196616 | tf_op jit(solution)/shard_map/ppermute | solution.py:773
  246.7 8.7 %copy-start.25 = (bf16[64,512]{1,0:T(8,128)(2,1)}, bf16[64,512]{1,0:T(8,128)(2,1)S(1)}, u32[]{:S(2)}) copy-start(bf16[64,512]{1,0:T(8,128)(2,1)S(1)} %collective-permute-done.28.a_one) | copy-start | bytes 196612
  246.7 5.2 %collective-permute-start.30 = (bf16[64,512]{1,0:T(8,128)(2,1)S(1)}, bf16[64,512]{1,0:T(8,128)(2,1)S(1)}, u32[]{:S(2)}, u32[]{:S(2)}) collective-permute-start(bf16[64,512]{1,0:T(8,128)(2,1)S(1)} %get-tuple-element.83), channel_id=1, source_target_pairs={{0,17},{1,16},{2,19},{3,18},{4,21},{5,20},{6,23},{7,22},{8,25},{9,... | collective-permute-start | bytes 196616 | tf_op jit(solution)/shard_map/ppermute | solution.py:773
  258.6 1.4 collective-permute-start.34
  260.7 3.6 %collective-permute-start.35 = (f32[8,128]{1,0:T(8,128)S(1)}, f32[8,128]{1,0:T(8,128)S(1)}, u32[]{:S(2)}, u32[]{:S(2)}) collective-permute-start(f32[8,128]{1,0:T(8,128)S(1)} %add.132), channel_id=1, source_target_pairs={{0,16},{1,17},{2,18},{3,19},{4,20},{5,21},{6,22},{7,23},{8,24},{9,... | collective-permute-start | bytes 12296 | tf_op jit(solution)/shard_map/ppermute | solution.py:773
  261.7 3.6 %collective-permute-start.36 = (f32[8,128]{1,0:T(8,128)S(1)}, f32[8,128]{1,0:T(8,128)S(1)}, u32[]{:S(2)}, u32[]{:S(2)}) collective-permute-start(f32[8,128]{1,0:T(8,128)S(1)} %add.132), channel_id=1, source_target_pairs={{0,1},{1,0},{2,3},{3,2},{4,5},{5,4},{6,7},{7,6},{8,9},{9,8},{10,11... | collective-permute-start | bytes 12296 | tf_op jit(solution)/shard_map/ppermute | solution.py:773
  262.7 4.5 %collective-permute-start.37 = (f32[8,128]{1,0:T(8,128)S(1)}, f32[8,128]{1,0:T(8,128)S(1)}, u32[]{:S(2)}, u32[]{:S(2)}) collective-permute-start(f32[8,128]{1,0:T(8,128)S(1)} %add.132), channel_id=1, source_target_pairs={{0,17},{1,16},{2,19},{3,18},{4,21},{5,20},{6,23},{7,22},{8,25},{9,... | collective-permute-start | bytes 12296 | tf_op jit(solution)/shard_map/ppermute | solution.py:773
  267.2 6.2 %collective-permute-start.38 = (f32[8,128]{1,0:T(8,128)S(1)}, f32[8,128]{1,0:T(8,128)S(1)}, u32[]{:S(2)}, u32[]{:S(2)}) collective-permute-start(f32[8,128]{1,0:T(8,128)S(1)} %add_add_fusion.1), channel_id=1, source_target_pairs={{0,2},{1,3},{2,0},{3,1},{4,6},{5,7},{6,4},{7,5},{8,10},{9,11},{10,... | collective-permute-start | bytes 12296 | tf_op jit(solution)/shard_map/ppermute | solution.py:773
  269.7 4.5 %collective-permute-start.39 = (f32[8,128]{1,0:T(8,128)S(1)}, f32[8,128]{1,0:T(8,128)S(1)}, u32[]{:S(2)}, u32[]{:S(2)}) collective-permute-start(f32[8,128]{1,0:T(8,128)S(1)} %add_add_fusion.1), channel_id=1, source_target_pairs={{0,4},{1,5},{2,6},{3,7},{4,0},{5,1},{6,2},{7,3},{8,12},{9,13},{10,... | collective-permute-start | bytes 12296 | tf_op jit(solution)/shard_map/ppermute | solution.py:773
  270.4 5.4 %collective-permute-start.40 = (f32[8,128]{1,0:T(8,128)S(1)}, f32[8,128]{1,0:T(8,128)S(1)}, u32[]{:S(2)}, u32[]{:S(2)}) collective-permute-start(f32[8,128]{1,0:T(8,128)S(1)} %add_add_fusion.1), channel_id=1, source_target_pairs={{0,6},{1,7},{2,4},{3,5},{4,2},{5,3},{6,0},{7,1},{8,14},{9,15},{10,... | collective-permute-start | bytes 12296 | tf_op jit(solution)/shard_map/ppermute | solution.py:773
  (21 other events, 73.9 us)
